TPU v7x, 32 devices: a whole 2x2x4 slice. The times are simulated.
32 devices in a mesh: cond: 2 (over core), kern: 2 (over y), tile: 8 (over z, x).
Axes of the slice: x: 2, y: 2, z: 4, core: 2. Of those that a mesh axis runs over, the one named last changes fastest.
Arguments:
- mask: bfloat16 [1, 1024, 1024], P(None, 'tile'), may hold values from -6 to 6
- kernels: bfloat16 [2, 4, 24, 512, 512], P(None, 'cond', 'kern', 'tile'), may hold values from -6 to 6
- kernel_weights: float32 [4, 24], P('cond', 'kern'), may hold values from 0.02 to 0.2
Outputs:
- low: float32 [1, 1024, 1024], P(None, 'tile', 'kern')
- high: float32 [1, 1024, 1024], P(None, 'tile', 'kern')
All inputs are finite; a program needn't handle non-finite values.
Results may differ from a plain program's by a relative error of at most 0.0032.
Values may be sent and summed in bfloat16 or wider, within the bound.
A program may use at most 128 MiB of HBM per device.

v0:
```python
import functools
import math

import jax
import jax.numpy as jnp
import numpy as np
from jax import lax
from jax.experimental import pallas as pl
from jax.experimental.pallas import tpu as pltpu
from jax.sharding import PartitionSpec as P


def tables(length, count):
    pixel = jnp.arange(length, dtype=jnp.int32)[:, None]
    freq = jnp.arange(count, dtype=jnp.int32)[None, :] - count // 2
    phase = jnp.mod(pixel * freq, length).astype(jnp.float32) * (2.0 * math.pi / length)
    factor = 1.0 / math.sqrt(length)
    return (
        (jnp.cos(phase) * factor).astype(jnp.bfloat16),
        (jnp.sin(phase) * factor).astype(jnp.bfloat16),
    )


def field_power(half_re, half_im, cos_table, sin_table):
    field_re = jnp.einsum("tnjr,pj->tnrp", half_re, cos_table, preferred_element_type=jnp.float32)
    field_re = field_re - jnp.einsum(
        "tnjr,pj->tnrp", half_im, sin_table, preferred_element_type=jnp.float32
    )
    field_im = jnp.einsum("tnjr,pj->tnrp", half_re, sin_table, preferred_element_type=jnp.float32)
    field_im = field_im + jnp.einsum(
        "tnjr,pj->tnrp", half_im, cos_table, preferred_element_type=jnp.float32
    )
    return field_re * field_re + field_im * field_im


def filter_spectrum(spec_re, spec_im, kern_re, kern_im):
    kern_re = kern_re.astype(jnp.float32)
    kern_im = kern_im.astype(jnp.float32)
    filt_re = spec_re[:, None] * kern_re[None] - spec_im[:, None] * kern_im[None]
    filt_im = spec_re[:, None] * kern_im[None] + spec_im[:, None] * kern_re[None]
    return (filt_re.astype(jnp.bfloat16), filt_im.astype(jnp.bfloat16))


def half_transform(filt_re, filt_im, cos_part, sin_part):
    half_re = jnp.einsum("tnji,ri->tnjr", filt_re, cos_part, preferred_element_type=jnp.float32)
    half_re = half_re - jnp.einsum(
        "tnji,ri->tnjr", filt_im, sin_part, preferred_element_type=jnp.float32
    )
    half_im = jnp.einsum("tnji,ri->tnjr", filt_re, sin_part, preferred_element_type=jnp.float32)
    half_im = half_im + jnp.einsum(
        "tnji,ri->tnjr", filt_im, cos_part, preferred_element_type=jnp.float32
    )
    return (half_re.astype(jnp.bfloat16), half_im.astype(jnp.bfloat16))


def column_spectrum(rows_re, rows_im, cos_part, sin_part):
    spec_re = jnp.einsum("tjr,ri->tji", rows_re, cos_part, preferred_element_type=jnp.float32)
    spec_re = spec_re + jnp.einsum(
        "tjr,ri->tji", rows_im, sin_part, preferred_element_type=jnp.float32
    )
    spec_im = jnp.einsum("tjr,ri->tji", rows_im, cos_part, preferred_element_type=jnp.float32)
    spec_im = spec_im - jnp.einsum(
        "tjr,ri->tji", rows_re, sin_part, preferred_element_type=jnp.float32
    )
    return (spec_re, spec_im)


def local(mask, kernels, kernel_weights):
    tiles_here, rows, pixels = mask.shape
    count = kernels.shape[4]
    conds, kerns = kernel_weights.shape
    items = conds * kerns
    cos_table, sin_table = tables(pixels, count)
    row_re = jnp.einsum("trc,cj->tjr", mask, cos_table, preferred_element_type=jnp.float32).astype(
        jnp.bfloat16
    )
    row_im = (
        -jnp.einsum("trc,cj->tjr", mask, sin_table, preferred_element_type=jnp.float32)
    ).astype(jnp.bfloat16)
    cols_re, cols_im = (
        lax.all_to_all(row_re, "tile", split_axis=1, concat_axis=2, tiled=True),
        lax.all_to_all(row_im, "tile", split_axis=1, concat_axis=2, tiled=True),
    )
    spec_re, spec_im = column_spectrum(cols_re, cols_im, cos_table, sin_table)
    freq_here = kernels.shape[3]
    kern_re = kernels[0].reshape(items, freq_here, count)
    kern_im = kernels[1].reshape(items, freq_here, count)
    filt_re, filt_im = filter_spectrum(spec_re, spec_im, kern_re, kern_im)
    half_re, half_im = half_transform(filt_re, filt_im, cos_table, sin_table)
    power = field_power(
        lax.all_to_all(half_re, "tile", split_axis=3, concat_axis=2, tiled=True),
        lax.all_to_all(half_im, "tile", split_axis=3, concat_axis=2, tiled=True),
        cos_table,
        sin_table,
    )
    power = power.reshape(tiles_here, conds, kerns, rows, pixels)
    weighted = jnp.einsum("tckrp,ck->tcrp", power, kernel_weights, precision=lax.Precision.HIGHEST)
    intensity = lax.psum_scatter(weighted, "kern", scatter_dimension=3, tiled=True)
    local_low = jnp.min(intensity, axis=1)
    local_high = jnp.max(intensity, axis=1)
    low = lax.pmin(local_low, "cond")
    high = lax.pmax(local_high, "cond")
    return (low, high)


def host_tables(length, count):
    pixel = np.arange(length, dtype=np.int64)[:, None]
    freq = np.arange(count, dtype=np.int64)[None, :] - count // 2
    phase = np.mod(pixel * freq, length).astype(np.float64) * (2.0 * math.pi / length)
    factor = 1.0 / math.sqrt(length)
    return np.cos(phase) * factor, np.sin(phase) * factor


def filter_kernel(core_ref, spec_ref, kept_ref, came_ref, out_ref):
    freqs, count = spec_ref.shape[1:]
    half = freqs // 2
    row = lax.broadcasted_iota(jnp.int32, (freqs, freqs), 0)
    col = lax.broadcasted_iota(jnp.int32, (freqs, freqs), 1)
    source = jnp.where(row < half, 2 * row, 2 * (row - half) + 1)
    order = (col == source).astype(jnp.bfloat16)
    spec_re = spec_ref[0]
    spec_im = spec_ref[1]

    def apply(kern_ref):
        chunks = kern_ref.shape[2]
        for part in range(kern_ref.shape[1] * chunks):
            kern_re = kern_ref[0, part // chunks, part % chunks].astype(jnp.float32)
            kern_im = kern_ref[1, part // chunks, part % chunks].astype(jnp.float32)
            filt_re = (spec_re * kern_re - spec_im * kern_im).astype(jnp.bfloat16)
            filt_im = (spec_re * kern_im + spec_im * kern_re).astype(jnp.bfloat16)
            out_ref[part, 0] = jnp.dot(order, filt_re, preferred_element_type=jnp.float32).astype(
                jnp.bfloat16
            )
            out_ref[part, 1] = jnp.dot(order, filt_im, preferred_element_type=jnp.float32).astype(
                jnp.bfloat16
            )

    mine = pl.program_id(0) == core_ref[0]

    @pl.when(mine)
    def _():
        apply(kept_ref)

    @pl.when(jnp.logical_not(mine))
    def _():
        apply(came_ref)


def filter_round(core, spec, kernels, came, which):
    _, conds, _, chunks, _, freqs, count = kernels.shape
    owners = conds * chunks
    mine = pl.BlockSpec(
        (2, conds, None, chunks, None, freqs, count),
        lambda b, own: (0, 0, own[0], 0, which, 0, 0),
    )
    return pl.pallas_call(
        filter_kernel,
        grid_spec=pltpu.PrefetchScalarGridSpec(
            num_scalar_prefetch=1,
            grid=(2,),
            in_specs=[pl.BlockSpec((2, freqs, count), lambda b, own: (0, 0, 0)), mine, mine],
            out_specs=pl.BlockSpec((owners, 2, freqs, count), lambda b, own: (b, 0, 0, 0)),
        ),
        out_shape=jax.ShapeDtypeStruct((2 * owners, 2, freqs, count), jnp.bfloat16),
        cost_estimate=pl.CostEstimate(
            flops=32 * owners * freqs * freqs * count,
            bytes_accessed=16 * owners * freqs * count,
            transcendentals=0,
        ),
    )(core, spec, kernels, came)


def item_kernel(first, last, weight_ref, parts_ref, wave_ref, back_ref, *rest):
    if first:
        out_ref, mixed, turn = rest
        sum_ref = None
    else:
        sum_ref, out_ref, mixed, turn = rest
    owners, _, freqs, count = parts_ref.shape
    half = freqs // 2
    quarter = count // 2
    width = back_ref.shape[2]

    @pl.when(pl.program_id(0) == 0)
    def _():
        for parity in range(2):
            base = parity * count
            for owner in range(owners):
                at = base + owner * half
                re = parts_ref[owner, 0, parity * half : (parity + 1) * half, :]
                im = parts_ref[owner, 1, parity * half : (parity + 1) * half, :]
                mixed[at : at + half, :count] = re
                mixed[at : at + half, count:] = -im
                mixed[at + quarter : at + quarter + half, :count] = im
                mixed[at + quarter : at + quarter + half, count:] = re
            cos_part = back_ref[2 * parity]
            sin_part = back_ref[2 * parity + 1]
            turn[parity, :quarter, :width] = cos_part
            turn[parity, :quarter, width:] = sin_part
            turn[parity, quarter:, :width] = -sin_part
            turn[parity, quarter:, width:] = cos_part

    halves = lax.dot_general(
        wave_ref[...], mixed[...], (((1,), (1,)), ((), ())), preferred_element_type=jnp.float32
    ).astype(jnp.bfloat16)
    even = jnp.dot(halves[:, :count], turn[0], preferred_element_type=jnp.float32)
    odd = jnp.dot(halves[:, count:], turn[1], preferred_element_type=jnp.float32)
    near = even + odd
    far = even - odd
    weight = weight_ref[0]
    powers = []
    for index, field in enumerate((near, far)):
        re = field[:, :width]
        im = field[:, width:]
        power = weight * (re * re + im * im)
        if not first:
            power = power + sum_ref[:, index * width : (index + 1) * width]
        powers.append(power)
    if not last:
        for index, power in enumerate(powers):
            out_ref[:, index * width : (index + 1) * width] = power
    else:
        total = jnp.concatenate(powers, axis=1)
        across, tall, rows, wide = out_ref.shape
        for k in range(across):
            for t in range(tall):
                out_ref[k, t] = total[t * rows : (t + 1) * rows, k * wide : (k + 1) * wide].astype(
                    out_ref.dtype
                )


def item_round(weight, parts, wave, back, total, last, blocks):
    pixels = wave.shape[0]
    owners, _, freqs, count = parts.shape
    kern, tile = blocks
    rows = pixels // tile
    tall = max(1, 256 // rows)
    step = tall * rows
    steps = pixels // step
    first = total is None
    in_specs = [
        pl.BlockSpec(memory_space=pltpu.SMEM),
        pl.BlockSpec(parts.shape, lambda b: (0, 0, 0, 0)),
        pl.BlockSpec((step, 2 * count), lambda b: (b, 0)),
        pl.BlockSpec(back.shape, lambda b: (0, 0, 0)),
    ]
    args = [weight, parts, wave, back]
    if not first:
        in_specs.append(pl.BlockSpec((step, pixels), lambda b: (b, 0)))
        args.append(total)
    if last:
        out_shape = jax.ShapeDtypeStruct((kern, tile, rows, pixels // kern), jnp.bfloat16)
        out_spec = pl.BlockSpec((kern, tall, rows, pixels // kern), lambda b: (0, b, 0, 0))
    else:
        out_shape = jax.ShapeDtypeStruct((pixels, pixels), jnp.float32)
        out_spec = pl.BlockSpec((step, pixels), lambda b: (b, 0))
    return pl.pallas_call(
        functools.partial(item_kernel, first, last),
        grid=(steps,),
        out_shape=out_shape,
        in_specs=in_specs,
        out_specs=out_spec,
        scratch_shapes=[
            pltpu.VMEM((2 * count, 2 * count), jnp.bfloat16),
            pltpu.VMEM((2, count, pixels), jnp.bfloat16),
        ],
        compiler_params=pltpu.CompilerParams(vmem_limit_bytes=48 * 1024 * 1024),
        cost_estimate=pl.CostEstimate(
            flops=2 * pixels * 4 * count * count + 4 * pixels * pixels * count,
            bytes_accessed=4 * pixels * pixels + 4 * owners * freqs * count,
            transcendentals=0,
        ),
    )(*args)


def local_items(sizes, mask, kernels, kernel_weights):
    tile, kern, cond = sizes
    _, rows, pixels = mask.shape
    freqs, count = kernels.shape[3:]
    conds, kerns = kernel_weights.shape
    items = conds * kerns
    each = items // tile
    cos, sin = host_tables(pixels, count)
    wave = lax.optimization_barrier(
        jnp.asarray(np.concatenate([cos, sin], axis=1), jnp.bfloat16)
    )
    back = jnp.asarray(
        np.stack([part[: pixels // 2, parity::2].T for parity in range(2) for part in (cos, sin)]),
        jnp.bfloat16,
    )
    me = lax.axis_index("tile")
    core = lax.axis_index("cond")
    swap = [(source, 1 - source) for source in range(2)]
    part = kerns // 2
    shares = kernels.reshape(2, conds, 2, part // each, each, freqs, count)
    came = lax.ppermute(kernels, "cond", swap).reshape(shares.shape)
    other = lax.ppermute(kernel_weights, "cond", swap)
    weights = jnp.where(
        core == 0,
        jnp.concatenate([kernel_weights, other]),
        jnp.concatenate([other, kernel_weights]),
    )
    weights = lax.dynamic_slice(weights, (0, core * part), (2 * conds, part)).reshape(items)
    weights = lax.dynamic_slice(weights, (me * each,), (each,))
    row = lax.optimization_barrier(jnp.dot(mask[0], wave, preferred_element_type=jnp.float32))
    row = row.reshape(rows, 2, tile, freqs)
    sign = jnp.asarray([1.0, -1.0], jnp.float32).reshape(1, 2, 1, 1)
    row = (row * sign).astype(jnp.bfloat16)
    row = row.transpose(2, 0, 1, 3).reshape(tile, rows, 2 * freqs)
    cols = lax.all_to_all(row, "tile", split_axis=0, concat_axis=0, tiled=True)
    cols = cols.reshape(pixels, 2 * freqs)
    mixed = lax.dot_general(
        cols, wave, (((0,), (0,)), ((), ())), preferred_element_type=jnp.float32
    )
    spec = jnp.stack(
        [
            mixed[:freqs, :count] + mixed[freqs:, count:],
            mixed[freqs:, :count] - mixed[:freqs, count:],
        ]
    )
    arrived = []
    for index in range(each):
        sent = filter_round(core.reshape(1), spec, shares, came, index)
        arrived.append(lax.all_to_all(sent, "tile", split_axis=0, concat_axis=0, tiled=True))
    total = None
    for index in range(each):
        total = item_round(
            weights[index : index + 1],
            arrived[index],
            wave,
            back,
            total,
            index == each - 1,
            (kern, tile),
        )
    wide = pixels // kern
    total = total.reshape(kern * tile, 2, rows // 2, wide)
    own = lax.dynamic_index_in_dim(total, core, 1, keepdims=False)
    sent = lax.dynamic_index_in_dim(total, 1 - core, 1, keepdims=False)
    got = lax.ppermute(sent, "cond", swap)
    total = (own.astype(jnp.float32) + got.astype(jnp.float32)).astype(jnp.bfloat16)
    blocks = lax.all_to_all(total, ("kern", "tile"), split_axis=0, concat_axis=0, tiled=True)
    blocks = blocks.reshape(kern, 2 * conds, tile // (2 * conds), rows // 2, wide)
    intensity = jnp.sum(blocks.astype(jnp.float32), axis=(0, 2))
    both = jnp.stack([jnp.min(intensity, axis=0), jnp.max(intensity, axis=0)])
    other = lax.ppermute(both, "cond", swap)
    upper = jnp.where(core == 0, both, other)
    lower = jnp.where(core == 0, other, both)
    low = jnp.concatenate([upper[0], lower[0]])
    high = jnp.concatenate([upper[1], lower[1]])
    return (low[None], high[None])


def plan(mesh):
    tile, kern, cond = (mesh.shape[name] for name in ("tile", "kern", "cond"))

    def body(mask, kernels, kernel_weights):
        conds, kerns = kernel_weights.shape
        freqs = kernels.shape[3]
        rows, pixels = mask.shape[1:]
        whole_items = cond == 2 and (conds * kerns) % tile == 0 and tile % (2 * conds) == 0
        whole_items = whole_items and (kerns // 2) % max(1, conds * kerns // tile) == 0
        aligned = freqs % 32 == 0 and rows % 32 == 0 and kerns % 2 == 0 and (pixels // kern) % 128 == 0
        if mask.shape[0] == 1 and whole_items and aligned and kernels.shape[4] * 2 == pixels:
            return local_items((tile, kern, cond), mask, kernels, kernel_weights)
        return local(mask, kernels, kernel_weights)

    return body


def solution(mesh):
    placed = (P(None, "tile", None), P(None, "cond", "kern", "tile", None), P("cond", "kern"))
    return jax.shard_map(
        plan(mesh),
        mesh=mesh,
        in_specs=placed,
        out_specs=(P(None, "tile", "kern"), P(None, "tile", "kern")),
        check_vma=False,
    )
```

profile of v0, /device:TPU:0, one launch (start us, length us, event | category | flops | bytes accessed | tf_op | source)
XLA Modules:
  0.0 162.4 jit_solution(6823906165216596013)
XLA Ops:
  1.6 2.5 %convolution_bitcast_fusion = f32[128,1024]{0,1:T(8,128)S(1)} fusion(bf16[1024,1024]{1,0:T(8,128)(2,1)} %constant.42.clone.wave_ref, bf16[1,128,1024]{2,1,0:T(8,128)(2,1)S(1)} %copy-done), kind=kOutput, calls=%fused_computation.3 | convolution fusion | flops 268435456 | bytes 2883584 | tf_op jit(solution)/shard_map/dot_general | solution.py:305
  4.1 0.8 fusion.1
  4.9 7.3 %all-to-all-start = ((bf16[8,128,128]{1,2,0:T(8,128)(2,1)}), bf16[8,128,128]{1,2,0:T(8,128)(2,1)S(1)}, u32[]{:S(2)}, u32[]{:S(2)}) async-start(bf16[8,128,128]{1,2,0:T(8,128)(2,1)} %bitcast.5), calls=%async_computation | async-start | bytes 524288 | tf_op jit(solution)/shard_map/all_to_all | solution.py:310
  12.2 8.9 %all-to-all-done = bf16[8,128,128]{1,2,0:T(8,128)(2,1)S(1)} async-done(((bf16[8,128,128]{1,2,0:T(8,128)(2,1)}), bf16[8,128,128]{1,2,0:T(8,128)(2,1)S(1)}, u32[]{:S(2)}, u32[]{:S(2)}) %all-to-all-start) | async-done | bytes 262176 | tf_op jit(solution)/shard_map/all_to_all | solution.py:310
  21.8 0.7 pad_maximum_fusion.spec_ref
  22.5 2.9 %shard_map.78 = bf16[8,2,64,512]{3,2,1,0:T(8,128)(2,1)} custom-call(s32[1]{0:T(128)} %bitcast.core_ref, f32[2,64,512]{2,1,0:T(8,128)} %pad_maximum_fusion.spec_ref, bf16[2,2,2,2,3,64,512]{6,5,4,3,2,1,0:T(8,128)(2,1)} %bitcast.44, bf16[2,2,2,2,3,64,512]{6,5,4,3,2,1,0:T(8,128)(2,1)} %bitcast.10.came_ref), custom_call_target="tpu_custom_call" | custom-call | flops 268435456 | bytes 2097152 | tf_op jit(solution)/shard_map/pallas_call | solution.py:156
  25.4 3.6 %all-to-all-start.2 = ((bf16[8,2,64,512]{3,2,1,0:T(8,128)(2,1)}), bf16[8,2,64,512]{3,2,1,0:T(8,128)(2,1)S(1)}, u32[]{:S(2)}, u32[]{:S(2)}) async-start(bf16[8,2,64,512]{3,2,1,0:T(8,128)(2,1)} %shard_map.78), calls=%async_computation.2 | async-start | bytes 2097152 | tf_op jit(solution)/shard_map/all_to_all | solution.py:324
  29.0 2.9 %shard_map.79 = bf16[8,2,64,512]{3,2,1,0:T(8,128)(2,1)} custom-call(s32[1]{0:T(128)} %bitcast.core_ref, f32[2,64,512]{2,1,0:T(8,128)} %pad_maximum_fusion.spec_ref, bf16[2,2,2,2,3,64,512]{6,5,4,3,2,1,0:T(8,128)(2,1)} %bitcast.45, bf16[2,2,2,2,3,64,512]{6,5,4,3,2,1,0:T(8,128)(2,1)} %bitcast.10.came_ref), custom_call_target="tpu_custom_call" | custom-call | flops 268435456 | bytes 2097152 | tf_op jit(solution)/shard_map/pallas_call | solution.py:156
  31.9 22.6 %all-to-all-done.2.parts_ref = bf16[8,2,64,512]{3,2,1,0:T(8,128)(2,1)S(1)} async-done(((bf16[8,2,64,512]{3,2,1,0:T(8,128)(2,1)}), bf16[8,2,64,512]{3,2,1,0:T(8,128)(2,1)S(1)}, u32[]{:S(2)}, u32[]{:S(2)}) %all-to-all-start.2) | async-done | bytes 1048608 | tf_op jit(solution)/shard_map/all_to_all | solution.py:324
  54.6 4.3 %all-to-all-start.3 = ((bf16[8,2,64,512]{3,2,1,0:T(8,128)(2,1)}), bf16[8,2,64,512]{3,2,1,0:T(8,128)(2,1)}, u32[]{:S(2)}, u32[]{:S(2)}) async-start(bf16[8,2,64,512]{3,2,1,0:T(8,128)(2,1)} %shard_map.79), calls=%async_computation.3 | async-start | bytes 2097152 | tf_op jit(solution)/shard_map/all_to_all | solution.py:324
  58.8 3.0 %shard_map.77 = bf16[8,2,64,512]{3,2,1,0:T(8,128)(2,1)} custom-call(s32[1]{0:T(128)} %bitcast.core_ref, f32[2,64,512]{2,1,0:T(8,128)} %pad_maximum_fusion.spec_ref, bf16[2,2,2,2,3,64,512]{6,5,4,3,2,1,0:T(8,128)(2,1)} %bitcast.46, bf16[2,2,2,2,3,64,512]{6,5,4,3,2,1,0:T(8,128)(2,1)} %bitcast.10.came_ref), custom_call_target="tpu_custom_call" | custom-call | flops 268435456 | bytes 2097152 | tf_op jit(solution)/shard_map/pallas_call | solution.py:156
  61.8 22.5 %all-to-all-done.3.parts_ref = bf16[8,2,64,512]{3,2,1,0:T(8,128)(2,1)} async-done(((bf16[8,2,64,512]{3,2,1,0:T(8,128)(2,1)}), bf16[8,2,64,512]{3,2,1,0:T(8,128)(2,1)}, u32[]{:S(2)}, u32[]{:S(2)}) %all-to-all-start.3) | async-done | bytes 1048608 | tf_op jit(solution)/shard_map/all_to_all | solution.py:324
  84.3 4.2 %all-to-all-start.1 = ((bf16[8,2,64,512]{3,2,1,0:T(8,128)(2,1)}), bf16[8,2,64,512]{3,2,1,0:T(8,128)(2,1)}, u32[]{:S(2)}, u32[]{:S(2)}) async-start(bf16[8,2,64,512]{3,2,1,0:T(8,128)(2,1)} %shard_map.77), calls=%async_computation.1 | async-start | bytes 2097152 | tf_op jit(solution)/shard_map/all_to_all | solution.py:324
  88.6 1.1 collective-permute-done
  90.6 1.2 copy-done.2
  91.9 8.8 %shard_map.80.rest_0_ = f32[1024,1024]{1,0:T(8,128)} custom-call(f32[1]{0:T(128)} %get-tuple-element.12.weight_ref, bf16[8,2,64,512]{3,2,1,0:T(8,128)(2,1)} %all-to-all-done.3.parts_ref, bf16[1024,1024]{1,0:T(8,128)(2,1)S(1)} %copy-done.1, bf16[4,256,512]{2,1,0:T(8,128)(2,1)S(1)} %copy-done.2), custom_call_target="tpu_custom_call" | custom-call | flops 4294967296 | bytes 5242880 | tf_op jit(solution)/shard_map/pallas_call | solution.py:257
  100.6 9.0 %shard_map.81.rest_0_ = f32[1024,1024]{1,0:T(8,128)} custom-call(f32[1]{0:T(128)} %get-tuple-element.13.weight_ref, bf16[8,2,64,512]{3,2,1,0:T(8,128)(2,1)S(1)} %all-to-all-done.2.parts_ref, bf16[1024,1024]{1,0:T(8,128)(2,1)S(1)} %copy-done.1, bf16[4,256,512]{2,1,0:T(8,128)(2,1)S(1)} %copy-done.2, f32[1024,1024]{1,0:T(8,128)} %shard_map.80.rest_0_), custom_call_target="tpu_custom_call" | custom-call | flops 4294967296 | bytes 5242880 | tf_op jit(solution)/shard_map/pallas_call | solution.py:257
  109.7 4.2 %all-to-all-done.1.parts_ref = bf16[8,2,64,512]{3,2,1,0:T(8,128)(2,1)} async-done(((bf16[8,2,64,512]{3,2,1,0:T(8,128)(2,1)}), bf16[8,2,64,512]{3,2,1,0:T(8,128)(2,1)}, u32[]{:S(2)}, u32[]{:S(2)}) %all-to-all-start.1) | async-done | bytes 1048608 | tf_op jit(solution)/shard_map/all_to_all | solution.py:324
  113.9 1.2 copy-done.3
  115.2 8.5 %shard_map.82 = bf16[2,8,128,512]{3,2,1,0:T(8,128)(2,1)S(1)} custom-call(f32[1]{0:T(128)} %get-tuple-element.14.weight_ref, bf16[8,2,64,512]{3,2,1,0:T(8,128)(2,1)} %all-to-all-done.1.parts_ref, bf16[1024,1024]{1,0:T(8,128)(2,1)} %constant.42.clone.wave_ref, bf16[4,256,512]{2,1,0:T(8,128)(2,1)S(1)} %copy-done.3, f32[1024,1024]{1,0:T(8,128)} %shard_map.81.rest_0_), custom_call_target="tpu_custom_call" | custom-call | flops 4294967296 | bytes 5242880 | tf_op jit(solution)/shard_map/pallas_call | solution.py:257
  123.9 2.8 %collective-permute-done.2 = bf16[16,64,512]{2,1,0:T(8,128)(2,1)} collective-permute-done((bf16[16,64,512]{2,1,0:T(8,128)(2,1)S(1)}, bf16[16,64,512]{2,1,0:T(8,128)(2,1)}, u32[]{:S(2)}, u32[]{:S(2)}) %collective-permute-start.2) | collective-permute-done | bytes 1048608 | tf_op jit(solution)/shard_map/ppermute | solution.py:340
  126.6 1.5 fusion
  128.2 30.9 %all_to_all.25 = bf16[16,64,512]{2,1,0:T(8,128)(2,1)S(1)} all-to-all(bf16[16,64,512]{2,1,0:T(8,128)(2,1)S(1)} %fusion), channel_id=1, replica_groups=mesh['cond'=2,'kern'=2,'tile'=8] {'kern','tile'}, dimensions={0} | all-to-all | bytes 2097152 | tf_op jit(solution)/shard_map/all_to_all | solution.py:342
  159.4 1.5 collective-permute-done.3
  (31 shorter events, 4.6 us)
Async XLA Ops:
  0.6 1.0 copy-start
  0.6 3.4 %copy-start.5 = (f32[2]{0:T(128)S(1)}, f32[2]{0:T(128)}, u32[]{:S(2)}) copy-start(f32[2]{0:T(128)} %constant.44.clone) | copy-start | bytes 28
  0.7 21.9 %collective-permute-start.1 = (bf16[2,2,12,64,512]{4,3,2,1,0:T(8,128)(2,1)}, bf16[2,2,12,64,512]{4,3,2,1,0:T(8,128)(2,1)}, u32[]{:S(2)}, u32[]{:S(2)}) collective-permute-start(bf16[2,2,12,64,512]{4,3,2,1,0:T(8,128)(2,1)} %param.7), channel_id=1, source_target_pairs={{0,16},{16,0},{1,17},{17,1},{2,18},{18,2},{3,19},{19,3},{4,20},{20... | collective-permute-start | bytes 9437192 | tf_op jit(solution)/shard_map/ppermute | solution.py:296
  1.6 19.7 %copy-start.1 = (bf16[1024,1024]{1,0:T(8,128)(2,1)S(1)}, bf16[1024,1024]{1,0:T(8,128)(2,1)}, u32[]{:S(2)}) copy-start(bf16[1024,1024]{1,0:T(8,128)(2,1)} %constant.42.clone.wave_ref) | copy-start | bytes 6291460
  4.9 16.2 %all-to-all-start = ((bf16[8,128,128]{1,2,0:T(8,128)(2,1)}), bf16[8,128,128]{1,2,0:T(8,128)(2,1)S(1)}, u32[]{:S(2)}, u32[]{:S(2)}) async-start(bf16[8,128,128]{1,2,0:T(8,128)(2,1)} %bitcast.5), calls=%async_computation | async-start | bytes 524288 | tf_op jit(solution)/shard_map/all_to_all | solution.py:310
  25.4 29.1 %all-to-all-start.2 = ((bf16[8,2,64,512]{3,2,1,0:T(8,128)(2,1)}), bf16[8,2,64,512]{3,2,1,0:T(8,128)(2,1)S(1)}, u32[]{:S(2)}, u32[]{:S(2)}) async-start(bf16[8,2,64,512]{3,2,1,0:T(8,128)(2,1)} %shard_map.78), calls=%async_computation.2 | async-start | bytes 2097152 | tf_op jit(solution)/shard_map/all_to_all | solution.py:324
  54.6 29.7 %all-to-all-start.3 = ((bf16[8,2,64,512]{3,2,1,0:T(8,128)(2,1)}), bf16[8,2,64,512]{3,2,1,0:T(8,128)(2,1)}, u32[]{:S(2)}, u32[]{:S(2)}) async-start(bf16[8,2,64,512]{3,2,1,0:T(8,128)(2,1)} %shard_map.79), calls=%async_computation.3 | async-start | bytes 2097152 | tf_op jit(solution)/shard_map/all_to_all | solution.py:324
  61.8 26.7 %copy-start.4 = (f32[2,12]{1,0:T(2,128)S(1)}, f32[2,12]{1,0:T(2,128)}, u32[]{:S(2)}) copy-start(f32[2,12]{1,0:T(2,128)} %param.8) | copy-start | bytes 292
  84.3 29.6 %all-to-all-start.1 = ((bf16[8,2,64,512]{3,2,1,0:T(8,128)(2,1)}), bf16[8,2,64,512]{3,2,1,0:T(8,128)(2,1)}, u32[]{:S(2)}, u32[]{:S(2)}) async-start(bf16[8,2,64,512]{3,2,1,0:T(8,128)(2,1)} %shard_map.77), calls=%async_computation.1 | async-start | bytes 2097152 | tf_op jit(solution)/shard_map/all_to_all | solution.py:324
  88.5 1.2 collective-permute-start
  90.6 1.2 copy-start.2
  113.9 1.2 copy-start.3
  123.8 2.9 %collective-permute-start.2 = (bf16[16,64,512]{2,1,0:T(8,128)(2,1)S(1)}, bf16[16,64,512]{2,1,0:T(8,128)(2,1)}, u32[]{:S(2)}, u32[]{:S(2)}) collective-permute-start(bf16[16,64,512]{2,1,0:T(8,128)(2,1)S(1)} %dynamic-slice_bitcast_fusion), channel_id=1, source_target_pairs={{0,16},{16,0},{1,17},{17,1},{2,18},{18,2},{3,19},{19,3},{4,20},{20... | collective-permute-start | bytes 3145736 | tf_op jit(solution)/shard_map/ppermute | solution.py:340
  159.3 1.6 collective-permute-start.3
where the time goes:
time: 163 us; the launch traced here: 162 us
  waiting for transfers between devices  63.7 us (39%)
  Pallas kernels  35.1 us (22%)
  blocking collectives  30.9 us (19%)
  starting transfers between devices  20.1 us (12%)
  other arithmetic  4.86 us (3%)
  local copies, waits for them, and re-layouts  4.01 us (2%)
  matrix products  2.94 us (2%)
    all_to_all x3, waiting for transfers between devices, local_items(): lax.all_to_all(sent, 'tile', split_axis=0, concat_axis=0, tiled=True)  49.4 us
    all_to_all x1, blocking collectives, local_items(): lax.all_to_all(total, ('kern', 'tile'), split_axis=0, concat_axis=0, tile...  30.9 us
    pallas_call x3, Pallas kernels, item_round(): pl.pallas_call(functools.partial(item_kernel, first, last), grid=(steps,)...  26.3 us
    all_to_all x3, starting transfers between devices, local_items(): lax.all_to_all(sent, 'tile', split_axis=0, concat_axis=0, tiled=True)  12.1 us
    all_to_all x1, waiting for transfers between devices, local_items(): cols = lax.all_to_all(row, 'tile', split_axis=0, concat_axis=0, tiled=True)  8.92 us
    pallas_call x3, Pallas kernels, filter_round(): pl.pallas_call(filter_kernel, grid_spec=pltpu.PrefetchScalarGridSpec(num_...  8.77 us
    all_to_all x1, starting transfers between devices, local_items(): cols = lax.all_to_all(row, 'tile', split_axis=0, concat_axis=0, tiled=True)  7.28 us
  transfers between devices with their start and end apart: 8, of which 7 were waited for; matrix products, arithmetic and copies ran while one was open for 3% of the time, Pallas kernels for 15%

commit v1 on v0

v1 whole, which is shorter than its diff:
```python
import functools
import math

import jax
import jax.numpy as jnp
import numpy as np
from jax import lax
from jax.experimental import pallas as pl
from jax.experimental.pallas import tpu as pltpu
from jax.sharding import PartitionSpec as P


def tables(length, count):
    pixel = jnp.arange(length, dtype=jnp.int32)[:, None]
    freq = jnp.arange(count, dtype=jnp.int32)[None, :] - count // 2
    phase = jnp.mod(pixel * freq, length).astype(jnp.float32) * (2.0 * math.pi / length)
    factor = 1.0 / math.sqrt(length)
    return (
        (jnp.cos(phase) * factor).astype(jnp.bfloat16),
        (jnp.sin(phase) * factor).astype(jnp.bfloat16),
    )


def field_power(half_re, half_im, cos_table, sin_table):
    field_re = jnp.einsum("tnjr,pj->tnrp", half_re, cos_table, preferred_element_type=jnp.float32)
    field_re = field_re - jnp.einsum(
        "tnjr,pj->tnrp", half_im, sin_table, preferred_element_type=jnp.float32
    )
    field_im = jnp.einsum("tnjr,pj->tnrp", half_re, sin_table, preferred_element_type=jnp.float32)
    field_im = field_im + jnp.einsum(
        "tnjr,pj->tnrp", half_im, cos_table, preferred_element_type=jnp.float32
    )
    return field_re * field_re + field_im * field_im


def filter_spectrum(spec_re, spec_im, kern_re, kern_im):
    kern_re = kern_re.astype(jnp.float32)
    kern_im = kern_im.astype(jnp.float32)
    filt_re = spec_re[:, None] * kern_re[None] - spec_im[:, None] * kern_im[None]
    filt_im = spec_re[:, None] * kern_im[None] + spec_im[:, None] * kern_re[None]
    return (filt_re.astype(jnp.bfloat16), filt_im.astype(jnp.bfloat16))


def half_transform(filt_re, filt_im, cos_part, sin_part):
    half_re = jnp.einsum("tnji,ri->tnjr", filt_re, cos_part, preferred_element_type=jnp.float32)
    half_re = half_re - jnp.einsum(
        "tnji,ri->tnjr", filt_im, sin_part, preferred_element_type=jnp.float32
    )
    half_im = jnp.einsum("tnji,ri->tnjr", filt_re, sin_part, preferred_element_type=jnp.float32)
    half_im = half_im + jnp.einsum(
        "tnji,ri->tnjr", filt_im, cos_part, preferred_element_type=jnp.float32
    )
    return (half_re.astype(jnp.bfloat16), half_im.astype(jnp.bfloat16))


def column_spectrum(rows_re, rows_im, cos_part, sin_part):
    spec_re = jnp.einsum("tjr,ri->tji", rows_re, cos_part, preferred_element_type=jnp.float32)
    spec_re = spec_re + jnp.einsum(
        "tjr,ri->tji", rows_im, sin_part, preferred_element_type=jnp.float32
    )
    spec_im = jnp.einsum("tjr,ri->tji", rows_im, cos_part, preferred_element_type=jnp.float32)
    spec_im = spec_im - jnp.einsum(
        "tjr,ri->tji", rows_re, sin_part, preferred_element_type=jnp.float32
    )
    return (spec_re, spec_im)


def local(mask, kernels, kernel_weights):
    tiles_here, rows, pixels = mask.shape
    count = kernels.shape[4]
    conds, kerns = kernel_weights.shape
    items = conds * kerns
    cos_table, sin_table = tables(pixels, count)
    row_re = jnp.einsum("trc,cj->tjr", mask, cos_table, preferred_element_type=jnp.float32).astype(
        jnp.bfloat16
    )
    row_im = (
        -jnp.einsum("trc,cj->tjr", mask, sin_table, preferred_element_type=jnp.float32)
    ).astype(jnp.bfloat16)
    cols_re, cols_im = (
        lax.all_to_all(row_re, "tile", split_axis=1, concat_axis=2, tiled=True),
        lax.all_to_all(row_im, "tile", split_axis=1, concat_axis=2, tiled=True),
    )
    spec_re, spec_im = column_spectrum(cols_re, cols_im, cos_table, sin_table)
    freq_here = kernels.shape[3]
    kern_re = kernels[0].reshape(items, freq_here, count)
    kern_im = kernels[1].reshape(items, freq_here, count)
    filt_re, filt_im = filter_spectrum(spec_re, spec_im, kern_re, kern_im)
    half_re, half_im = half_transform(filt_re, filt_im, cos_table, sin_table)
    power = field_power(
        lax.all_to_all(half_re, "tile", split_axis=3, concat_axis=2, tiled=True),
        lax.all_to_all(half_im, "tile", split_axis=3, concat_axis=2, tiled=True),
        cos_table,
        sin_table,
    )
    power = power.reshape(tiles_here, conds, kerns, rows, pixels)
    weighted = jnp.einsum("tckrp,ck->tcrp", power, kernel_weights, precision=lax.Precision.HIGHEST)
    intensity = lax.psum_scatter(weighted, "kern", scatter_dimension=3, tiled=True)
    local_low = jnp.min(intensity, axis=1)
    local_high = jnp.max(intensity, axis=1)
    low = lax.pmin(local_low, "cond")
    high = lax.pmax(local_high, "cond")
    return (low, high)


def host_tables(length, count):
    pixel = np.arange(length, dtype=np.int64)[:, None]
    freq = np.arange(count, dtype=np.int64)[None, :] - count // 2
    phase = np.mod(pixel * freq, length).astype(np.float64) * (2.0 * math.pi / length)
    factor = 1.0 / math.sqrt(length)
    return np.cos(phase) * factor, np.sin(phase) * factor


MESH = pl.DeviceIdType.MESH


def fused_kernel(sizes, mask_ref, weight_ref, wave_hbm, kern_hbm, out_ref, *scratch):
    tile, kern, cond = sizes
    (wave, held, row_send, cols, spec, filt, recv, turn, back, half, grid, power, cross, pairs) = scratch[:14]
    (quarter_send, quarter_recv, plane_send, plane_recv, final) = scratch[14:19]
    (load_sem, row_out, row_in, pair_out, pair_in, send_out, send_in, pass_out, pass_in) = scratch[19:28]
    (quarter_out, quarter_in, plane_out, plane_in, final_out, final_in) = scratch[28:]
    rows, pixels = mask_ref.shape
    _, conds, kerns, freqs, count = kern_hbm.shape
    planes = conds * cond
    width = tile // planes
    items = kerns // width
    part = freqs // cond
    wide = back.shape[1] // 2
    lanes = pixels // 2
    side = lanes // width
    steps = back.shape[0]
    chunk = plane_recv.shape[2]
    subs = plane_recv.shape[1]
    me = lax.axis_index("tile")
    line = lax.axis_index("kern")
    core = lax.axis_index("cond")
    plane = lax.div(me, width)
    column = lax.rem(me, width)
    source = lax.div(plane, conds)

    def remote(src, dst, out_sem, in_sem, to_tile, to_line, to_core):
        return pltpu.make_async_remote_copy(
            src_ref=src,
            dst_ref=dst,
            send_sem=out_sem,
            recv_sem=in_sem,
            device_id={"tile": to_tile, "kern": to_line, "cond": to_core},
            device_id_type=MESH,
        )

    def arrived(ref, sem):
        pltpu.make_async_copy(ref, ref, sem).wait()

    wave_load = pltpu.make_async_copy(wave_hbm, wave, load_sem.at[0])
    kern_load = pltpu.make_async_copy(kern_hbm, held, load_sem.at[1])
    wave_load.start()
    kern_load.start()

    barrier = pltpu.get_barrier_semaphore()
    for step in range(tile - 1, 0, -1):
        for flip in range(cond):
            pl.semaphore_signal(
                barrier,
                inc=1,
                device_id={
                    "tile": lax.rem(me + step, tile),
                    "kern": line,
                    "cond": lax.rem(core + flip, cond),
                },
                device_id_type=MESH,
            )
    pl.semaphore_signal(
        barrier, inc=1, device_id={"tile": me, "kern": line, "cond": 1 - core}, device_id_type=MESH
    )
    for shift in range(width):
        pl.semaphore_signal(
            barrier,
            inc=1,
            device_id={
                "tile": plane * width + lax.rem(column + shift, width),
                "kern": 1 - line,
                "cond": core,
            },
            device_id_type=MESH,
        )
    greeted = (tile - 1) * cond + 1 + width

    wave_load.wait()
    row = jnp.dot(mask_ref[...], wave[...], preferred_element_type=jnp.float32).T
    row_send[:, :freqs, :] = row[:count].reshape(tile, freqs, rows).astype(jnp.bfloat16)
    row_send[:, freqs:, :] = (-row[count:]).reshape(tile, freqs, rows).astype(jnp.bfloat16)

    pl.semaphore_wait(barrier, greeted)
    place = cols.at[:, pl.ds(pl.multiple_of(me * rows, rows), rows)]
    pltpu.make_async_copy(row_send.at[me], place, row_in.at[me]).start()
    for step in range(tile - 1, 0, -1):
        to = lax.rem(me + step, tile)
        remote(
            row_send.at[to], place, row_out.at[step], row_in.at[me], to, line, core
        ).start()
    pair_copy = remote(
        weight_ref, pairs, pair_out.at[0], pair_in.at[0], me, line, 1 - core
    )
    pair_copy.start()

    for shift in range(width):
        for layer in range(planes // cond):
            at = pl.multiple_of(
                ((core * (planes // cond) + layer) * width + shift) * rows, rows
            )
            to = (shift * (planes // cond) + layer) * rows
            block = wave[pl.ds(at, rows), :].astype(jnp.float32).T.astype(jnp.bfloat16)
            turn[:count, to : to + rows] = block[:count]
            turn[:count, lanes + to : lanes + to + rows] = block[count:]
            turn[count:, to : to + rows] = -block[count:]
            turn[count:, lanes + to : lanes + to + rows] = block[:count]
    for step in range(steps):
        back[step, :wide, :] = wave[step * wide : (step + 1) * wide, :count]
        back[step, wide:, :] = wave[step * wide : (step + 1) * wide, count:]
    pack = 16
    first = lax.broadcasted_iota(jnp.int32, (pack, count), 0) == 0
    middle = jnp.broadcast_to(
        wave[pixels // 2 : pixels // 2 + pack, :count].astype(jnp.float32)[:1], (pack, count)
    )
    back[0, wide : wide + pack, :] = jnp.where(
        first, middle, wave[:pack, count:].astype(jnp.float32)
    ).astype(jnp.bfloat16)
    power[...] = jnp.zeros_like(power)
    cross[...] = jnp.zeros_like(cross)

    for step in range(tile):
        to = lax.rem(me + step, tile)
        arrived(cols.at[:, pl.ds(pl.multiple_of(to * rows, rows), rows)], row_in.at[to])
    mixed = jnp.dot(cols[...], wave[...], preferred_element_type=jnp.float32)
    spec[0] = mixed[:freqs, :count] + mixed[freqs:, count:]
    spec[1] = mixed[freqs:, :count] - mixed[:freqs, count:]
    kern_load.wait()

    def targets():
        for layer in range(conds):
            for shift in range(width):
                for other in range(cond):
                    index = (layer * width + shift) * cond + other
                    to = (core * conds + layer) * width + shift
                    yield index, layer, shift, other, to, jnp.logical_and(to == me, other == core)

    def filter_item(item):
        for layer in range(conds):
            for shift in range(width):
                slot = shift * items + item
                for at in range(0, freqs, pack):
                    near = pl.ds(at, pack)
                    kern_re = held[0, layer, slot, near, :].astype(jnp.float32)
                    kern_im = held[1, layer, slot, near, :].astype(jnp.float32)
                    spec_re = spec[0, near, :]
                    spec_im = spec[1, near, :]
                    filt[layer, slot, near, :count] = (
                        spec_re * kern_re - spec_im * kern_im
                    ).astype(jnp.bfloat16)
                    filt[layer, slot, near, count:] = (
                        spec_re * kern_im + spec_im * kern_re
                    ).astype(jnp.bfloat16)

    def send_item(item):
        for index, layer, shift, other, to, mine in targets():
            src = filt.at[layer, shift * items + item, pl.ds(other * part, part)]
            dst = recv.at[item, me, pl.ds(other * part, part)]

            @pl.when(mine)
            def _():
                pltpu.make_async_copy(src, dst, send_in.at[item, me]).start()

            @pl.when(jnp.logical_not(mine))
            def _():
                remote(
                    src, dst, send_out.at[item, index], send_in.at[item, me], to, line, other
                ).start()

    filter_item(0)

    def source_step(item, carry):
        filter_item(item)
        send_item(item - 1)
        return carry

    lax.fori_loop(1, items, source_step, 0)
    send_item(items - 1)

    pair_copy.wait()
    weights = jnp.where(source == core, weight_ref[...], pairs[...])
    lane = lax.broadcasted_iota(jnp.int32, weights.shape, 1)
    level = lax.broadcasted_iota(jnp.int32, weights.shape, 0)
    weights = jnp.where(level == lax.rem(plane, conds), weights, 0.0)
    sign = jnp.where(line == 0, 2.0, -2.0)
    mine_half = pl.ds(pl.multiple_of(core * part, part), part)
    their_half = pl.ds(pl.multiple_of((1 - core) * part, part), part)

    def passed(item, origin):
        return remote(
            recv.at[item, origin, mine_half],
            recv.at[item, origin, mine_half],
            pass_out.at[item, origin],
            pass_in.at[item, origin],
            me,
            line,
            1 - core,
        )

    peers = []
    for turn_x in range(width):
        for turn_y in range(kern):
            if turn_x or turn_y:
                peers.append((turn_x, turn_y))

    def quarter(index, piece):
        turn_x, turn_y = peers[index]
        to_column = lax.rem(column + turn_x, width)
        to_line = lax.rem(line + turn_y, kern)
        span = pl.ds(piece * chunk, chunk)
        return remote(
            quarter_send.at[to_line, to_column, span],
            quarter_recv.at[index, span],
            quarter_out.at[piece, index],
            quarter_in.at[piece, index],
            plane * width + to_column,
            to_line,
            core,
        )

    def item_step(item, carry):
        for origin in range(tile):
            arrived(recv.at[item, origin, mine_half], send_in.at[item, origin])
            passed(item, origin).start()
        for origin in range(tile):
            arrived(recv.at[item, origin, their_half], pass_in.at[item, origin])
        half[...] = jnp.dot(
            recv[item].reshape(count, 2 * count), turn[...], preferred_element_type=jnp.float32
        ).astype(jnp.bfloat16)
        weight = jnp.sum(jnp.where(lane == column * items + item, weights, 0.0))

        def pixel_step(step, carry):
            grid[...] = jnp.dot(back[step], half[...], preferred_element_type=jnp.float32)

            def group(at, carry):
                near = pl.ds(pl.multiple_of(at * pack, pack), pack)
                far = pl.ds(pl.multiple_of(wide + at * pack, pack), pack)
                a_re = grid[near, :lanes]
                a_im = grid[near, lanes:]
                b_re = grid[far, :lanes]
                b_im = grid[far, lanes:]
                into = pl.ds(pl.multiple_of(step * wide + at * pack, pack), pack)
                power[into, :] += weight * (
                    (a_re * a_re + a_im * a_im) + (b_re * b_re + b_im * b_im)
                )
                cross[into, :] += weight * (a_im * b_re - a_re * b_im)
                return carry

            lax.fori_loop(0, wide // pack, group, 0)

            @pl.when(step == 0)
            def _():
                top = 8
                a_re = grid[:top, :lanes]
                a_im = grid[:top, lanes:]
                b_re = grid[wide : wide + top, :lanes]
                b_im = grid[wide : wide + top, lanes:]
                a = a_re * a_re + a_im * a_im
                b = b_re * b_re + b_im * b_im
                only = lax.broadcasted_iota(jnp.int32, (top, lanes), 0) == 0
                power[:top, :] -= jnp.where(only, (0.5 * weight) * (a + b), 0.0)
                cross[:top, :] += jnp.where(
                    only, weight * (0.25 * (a - b) - (a_im * b_re - a_re * b_im)), 0.0
                )

            @pl.when(item == items - 1)
            def _():
                for piece in range(wide // chunk):

                    def finish(at, carry):
                        into = pl.ds(
                            pl.multiple_of(step * wide + piece * chunk + at * pack, pack), pack
                        )
                        total = power[into, :]
                        twice = 2.0 * cross[into, :]
                        for shift in range(width):
                            own = slice(shift * side, (shift + 1) * side)
                            quarter_send[0, shift, into, :] = (
                                total[:, own] + twice[:, own]
                            ).astype(jnp.bfloat16)
                            quarter_send[1, shift, into, :] = (
                                total[:, own] - twice[:, own]
                            ).astype(jnp.bfloat16)
                        return carry

                    lax.fori_loop(0, chunk // pack, finish, 0)
                    for index in range(len(peers)):
                        quarter(index, step * (wide // chunk) + piece).start()

            return carry

        lax.fori_loop(0, steps, pixel_step, 0)
        return carry

    lax.fori_loop(0, items, item_step, 0)

    def to_plane(layer, piece):
        other = piece // subs
        return (
            plane_send.at[layer, pl.ds(piece * chunk, chunk)],
            plane_recv.at[plane, piece % subs],
            plane_out.at[layer, piece],
            plane_in.at[plane, piece % subs],
            (core * (planes // cond) + layer) * width + column,
            line,
            other,
        )

    def own_plane(layer, piece):
        return jnp.logical_and(
            core * (planes // cond) + layer == plane, piece // subs == core
        )

    pieces = subs * cond
    own_side = pl.ds(pl.multiple_of(column * side, side), side)
    for piece in range(pieces):
        for index in range(len(peers)):
            arrived(quarter_recv.at[index, pl.ds(piece * chunk, chunk)], quarter_in.at[piece, index])
        for at in range(piece * chunk, (piece + 1) * chunk, pack):
            span = pl.ds(at, pack)
            total = power[span, own_side] + sign * cross[span, own_side]
            for index in range(len(peers)):
                total = total + quarter_recv[index, span, :].astype(jnp.float32)
            for layer in range(planes // cond):
                plane_send[layer, span, :] = total[:, layer * rows : (layer + 1) * rows].astype(
                    jnp.bfloat16
                )
        for layer in range(planes // cond):
            src, dst, out_sem, in_sem, to, to_line, other = to_plane(layer, piece)

            @pl.when(own_plane(layer, piece))
            def _():
                pltpu.make_async_copy(src, dst, in_sem).start()

            @pl.when(jnp.logical_not(own_plane(layer, piece)))
            def _():
                remote(src, dst, out_sem, in_sem, to, to_line, other).start()

    def swap(sub):
        span = pl.ds(pl.multiple_of((core * subs + sub) * chunk, chunk), chunk)
        return remote(
            final.at[:, span], final.at[:, span], final_out.at[sub], final_in.at[sub], me, line, 1 - core
        )

    for sub in range(subs):
        for layer in range(planes):
            arrived(plane_recv.at[layer, sub], plane_in.at[layer, sub])
        for at in range(0, chunk, pack):
            values = [
                plane_recv[layer, sub, at : at + pack, :].astype(jnp.float32)
                for layer in range(planes)
            ]
            into = pl.ds(pl.multiple_of((core * subs + sub) * chunk + at, pack), pack)
            final[0, into, :] = functools.reduce(jnp.minimum, values)
            final[1, into, :] = functools.reduce(jnp.maximum, values)
        swap(sub).start()

    for step in range(1, tile):
        to = lax.rem(me + step, tile)
        pltpu.make_async_copy(row_send.at[to], row_send.at[to], row_out.at[step]).wait()

    def drain(item, carry):
        for index, layer, shift, other, to, mine in targets():
            src = filt.at[layer, shift * items + item, pl.ds(other * part, part)]

            @pl.when(jnp.logical_not(mine))
            def _():
                arrived(src, send_out.at[item, index])

        for origin in range(tile):
            arrived(recv.at[item, origin, mine_half], pass_out.at[item, origin])
        return carry

    lax.fori_loop(0, items, drain, 0)
    for piece in range(pieces):
        for index in range(len(peers)):
            quarter(index, piece).wait_send()
        for layer in range(planes // cond):

            @pl.when(jnp.logical_not(own_plane(layer, piece)))
            def _():
                arrived(plane_send.at[layer, pl.ds(piece * chunk, chunk)], plane_out.at[layer, piece])

    for sub in range(subs):
        their = pl.ds(pl.multiple_of(((1 - core) * subs + sub) * chunk, chunk), chunk)
        arrived(final.at[:, their], final_in.at[sub])
        swap(sub).wait_send()
    out_ref[...] = final[...]


def fused(sizes, mask, kernels, weights, wave):
    tile, kern, cond = sizes
    rows, pixels = mask.shape
    _, conds, kerns, freqs, count = kernels.shape
    planes = conds * cond
    width = tile // planes
    items = kerns // width
    lanes = pixels // 2
    wide = 256
    chunk = 128
    steps = lanes // wide
    pieces = lanes // chunk
    peers = width * kern - 1
    dma = pltpu.SemaphoreType.DMA
    return pl.pallas_call(
        functools.partial(fused_kernel, sizes),
        out_shape=jax.ShapeDtypeStruct((2, lanes, rows), jnp.float32),
        in_specs=[
            pl.BlockSpec(memory_space=pltpu.VMEM),
            pl.BlockSpec(memory_space=pltpu.VMEM),
            pl.BlockSpec(memory_space=pl.ANY),
            pl.BlockSpec(memory_space=pl.ANY),
        ],
        out_specs=pl.BlockSpec(memory_space=pltpu.VMEM),
        scratch_shapes=[
            pltpu.VMEM((pixels, 2 * count), jnp.bfloat16),
            pltpu.VMEM(kernels.shape, jnp.bfloat16),
            pltpu.VMEM((tile, 2 * freqs, rows), jnp.bfloat16),
            pltpu.VMEM((2 * freqs, pixels), jnp.bfloat16),
            pltpu.VMEM((2, freqs, count), jnp.float32),
            pltpu.VMEM((conds, kerns, freqs, 2 * count), jnp.bfloat16),
            pltpu.VMEM((items, tile, freqs, 2 * count), jnp.bfloat16),
            pltpu.VMEM((2 * count, pixels), jnp.bfloat16),
            pltpu.VMEM((steps, 2 * wide, count), jnp.bfloat16),
            pltpu.VMEM((count, pixels), jnp.bfloat16),
            pltpu.VMEM((2 * wide, pixels), jnp.float32),
            pltpu.VMEM((lanes, lanes), jnp.float32),
            pltpu.VMEM((lanes, lanes), jnp.float32),
            pltpu.VMEM(weights.shape, jnp.float32),
            pltpu.VMEM((kern, width, lanes, lanes // width), jnp.bfloat16),
            pltpu.VMEM((peers, lanes, lanes // width), jnp.bfloat16),
            pltpu.VMEM((planes // cond, lanes, rows), jnp.bfloat16),
            pltpu.VMEM((planes, pieces // cond, chunk, rows), jnp.bfloat16),
            pltpu.VMEM((2, lanes, rows), jnp.float32),
            dma((2,)),
            dma((tile,)),
            dma((tile,)),
            dma((1,)),
            dma((1,)),
            dma((items, tile)),
            dma((items, tile)),
            dma((items, tile)),
            dma((items, tile)),
            dma((pieces, peers)),
            dma((pieces, peers)),
            dma((planes // cond, pieces)),
            dma((planes, pieces // cond)),
            dma((pieces // cond,)),
            dma((pieces // cond,)),
        ],
        compiler_params=pltpu.CompilerParams(
            collective_id=0, has_side_effects=True, vmem_limit_bytes=60 * 1024 * 1024
        ),
    )(mask, weights, wave, kernels)


def place_kernel(final_ref, low_ref, high_ref):
    line = lax.axis_index("kern")
    size = final_ref.shape[1]
    slot = lax.broadcasted_iota(jnp.int32, (size, size), 0)
    pixel = lax.broadcasted_iota(jnp.int32, (size, size), 1)
    wanted = jnp.where(line == 0, pixel, jnp.where(pixel == 0, 0, size - pixel))
    order = (slot == wanted).astype(jnp.float32)
    for ref, index in ((low_ref, 0), (high_ref, 1)):
        ref[0] = lax.dot_general(
            final_ref[index],
            order,
            (((0,), (0,)), ((), ())),
            preferred_element_type=jnp.float32,
            precision=lax.Precision.HIGHEST,
        )


def planes_of(sizes, mask, kernels, kernel_weights):
    _, rows, pixels = mask.shape
    count = kernels.shape[4]
    conds, kerns = kernel_weights.shape
    cos, sin = host_tables(pixels, count)
    wave = jnp.asarray(np.concatenate([cos, sin], axis=1), jnp.bfloat16)
    weights = jnp.pad(kernel_weights, ((0, 8 - conds), (0, 128 - kerns)))
    final = fused(sizes, mask[0], kernels, weights, wave)
    shape = jax.ShapeDtypeStruct((1, rows, pixels // 2), jnp.float32)
    return pl.pallas_call(place_kernel, out_shape=(shape, shape))(final)


def plan(mesh):
    tile, kern, cond = (mesh.shape[name] for name in ("tile", "kern", "cond"))

    def body(mask, kernels, kernel_weights):
        conds, kerns = kernel_weights.shape
        freqs, count = kernels.shape[3:]
        rows, pixels = mask.shape[1:]
        split = kern == 2 and cond == 2 and conds == 2 and tile == 2 * conds * cond
        split = split and mask.shape[0] == 1 and count * 2 == pixels and kerns % 2 == 0
        split = split and rows == 128 and freqs % 32 == 0 and pixels == tile * rows
        if split and kerns <= 128 and count % 512 == 0:
            return planes_of((tile, kern, cond), mask, kernels, kernel_weights)
        return local(mask, kernels, kernel_weights)

    return body


def solution(mesh):
    placed = (P(None, "tile", None), P(None, "cond", "kern", "tile", None), P("cond", "kern"))
    return jax.shard_map(
        plan(mesh),
        mesh=mesh,
        in_specs=placed,
        out_specs=(P(None, "tile", "kern"), P(None, "tile", "kern")),
        check_vma=False,
    )
```

time: 163 us -> 115 us (0.71)
  Pallas kernels: 35.1 us -> 113 us
  waiting for transfers between devices: 63.7 us -> 0 us
  blocking collectives: 30.9 us -> 0 us
  starting transfers between devices: 20.1 us -> 0 us
  other arithmetic: 4.86 us -> 0 us
  matrix products: 2.94 us -> 0 us
  local copies, waits for them, and re-layouts: 4.01 us -> 1.28 us
    pallas_call x6 -> x2, Pallas kernels: 35.1 us -> 113 us  [the longest x1 110 us: fused(): pl.pallas_call(functools.partial(fused_kernel, sizes), out_shape=jax.Shap...]
    all_to_all x4 -> x0, waiting for transfers between devices: 58.3 us -> none  [the longest x3 49.4 us: local_items(): lax.all_to_all(sent, 'tile', split_axis=0, concat_axis=0, tiled=True)]
    all_to_all x1 -> x0, blocking collectives: 30.9 us -> none  [local_items(): lax.all_to_all(total, ('kern', 'tile'), split_axis=0, concat_axis=0, tile...]
    all_to_all x4 -> x0, starting transfers between devices: 19.3 us -> none  [the longest x3 12.1 us: local_items(): lax.all_to_all(sent, 'tile', split_axis=0, concat_axis=0, tiled=True)]
    ppermute x4 -> x0, waiting for transfers between devices: 5.44 us -> none  [the longest x1 2.78 us: local_items(): got = lax.ppermute(sent, 'cond', swap)]
    dot_general x2 -> x0, matrix products: 2.94 us -> none  [the longest x1 2.48 us: local_items(): jnp.dot(mask[0], wave, preferred_element_type=jnp.float32)]
    unnamed x12 -> x0, local copies, waits for them, and re-layouts: 2.84 us -> none
    convert_element_type x2 -> x0, other arithmetic: 2.37 us -> none  [the longest x1 1.54 us: local_items(): (own.astype(jnp.float32) + got.astype(jnp.float32)).astype(jnp.bfloat16)]
  transfers between devices with their start and end apart: 8 -> 0, of which waited for: 7 -> 0; matrix products, arithmetic and copies ran while one was open for 3% -> 0% of each run, Pallas kernels for 15% -> 0%
where the time goes in v1:
time: 115 us
  Pallas kernels  113 us (98%)
  local copies, waits for them, and re-layouts  1.28 us (1%)
    pallas_call x1, Pallas kernels, fused(): pl.pallas_call(functools.partial(fused_kernel, sizes), out_shape=jax.Shap...  110 us
    pallas_call x1, Pallas kernels, planes_of(): return pl.pallas_call(place_kernel, out_shape=(shape, shape))(final)  2.96 us

profile of v1, /device:TPU:0, one launch (start us, length us, event | category | flops | bytes accessed | tf_op | source)
XLA Modules:
  0.0 115.2 jit_solution(9359238888282644414)
XLA Ops:
  0.6 1.3 %pad.4.weight_ref = f32[8,128]{1,0:T(8,128)} pad(f32[2,12]{1,0:T(2,128)} %param.6, f32[]{:T(128)} %constant.4.clone.1), padding=0_6x0_116 | pad | bytes 4196 | tf_op jit(solution)/shard_map/jit(_pad)/pad | solution.py:590
  1.9 110.3 %shard_map.59.final_ref = f32[2,512,128]{2,1,0:T(8,128)} custom-call(bf16[128,1024]{1,0:T(8,128)(2,1)} %bitcast.1, f32[8,128]{1,0:T(8,128)} %pad.4.weight_ref, bf16[1024,1024]{1,0:T(8,128)(2,1)} %constant.5.clone.wave_hbm, bf16[2,2,12,64,512]{4,3,2,1,0:T(8,128)(2,1)} %kern_hbm.1), custom_call_target="tpu_custom_call" | custom-call | tf_op jit(solution)/shard_map/pallas_call | solution.py:515
  112.3 3.0 %shard_map.60 = (f32[1,128,512]{2,1,0:T(8,128)}, f32[1,128,512]{2,1,0:T(8,128)}) custom-call(f32[2,512,128]{2,1,0:T(8,128)} %shard_map.59.final_ref), custom_call_target="tpu_custom_call" | custom-call | tf_op jit(solution)/shard_map/pallas_call | solution.py:593

commit v2 on v1

--- a/solution.py
+++ b/solution.py
@@ -118,8 +118,11 @@
     tile, kern, cond = sizes
     (wave, held, row_send, cols, spec, filt, recv, turn, back, half, grid, power, cross, pairs) = scratch[:14]
     (quarter_send, quarter_recv, plane_send, plane_recv, final) = scratch[14:19]
+    weight = scratch[-1]
     (load_sem, row_out, row_in, pair_out, pair_in, send_out, send_in, pass_out, pass_in) = scratch[19:28]
-    (quarter_out, quarter_in, plane_out, plane_in, final_out, final_in) = scratch[28:]
+    (quarter_out, quarter_in, plane_out, plane_in, final_out, final_in, share_out, share_in) = (
+        scratch[28:-1]
+    )
     rows, pixels = mask_ref.shape
     _, conds, kerns, freqs, count = kern_hbm.shape
     planes = conds * cond
@@ -186,21 +189,40 @@
         )
     greeted = (tile - 1) * cond + 1 + width
 
+    weight[...] = jnp.zeros_like(weight)
+    weight[:conds, :kerns] = weight_ref[...]
     wave_load.wait()
     row = jnp.dot(mask_ref[...], wave[...], preferred_element_type=jnp.float32).T
-    row_send[:, :freqs, :] = row[:count].reshape(tile, freqs, rows).astype(jnp.bfloat16)
-    row_send[:, freqs:, :] = (-row[count:]).reshape(tile, freqs, rows).astype(jnp.bfloat16)
+    row_re = row[:count].reshape(tile, cond, part, rows).astype(jnp.bfloat16)
+    row_im = (-row[count:]).reshape(tile, cond, part, rows).astype(jnp.bfloat16)
+    row_send[:, :, :part, :] = row_re
+    row_send[:, :, part:, :] = row_im
 
     pl.semaphore_wait(barrier, greeted)
-    place = cols.at[:, pl.ds(pl.multiple_of(me * rows, rows), rows)]
-    pltpu.make_async_copy(row_send.at[me], place, row_in.at[me]).start()
+
+    def column_of(origin, side_of):
+        return cols.at[side_of, :, pl.ds(pl.multiple_of(origin * rows, rows), rows)]
+
+    def shared(origin):
+        return remote(
+            column_of(origin, core),
+            column_of(origin, core),
+            share_out.at[origin],
+            share_in.at[origin],
+            me,
+            line,
+            1 - core,
+        )
+
+    place = column_of(me, core)
+    pltpu.make_async_copy(row_send.at[me, core], place, row_in.at[me]).start()
     for step in range(tile - 1, 0, -1):
         to = lax.rem(me + step, tile)
         remote(
-            row_send.at[to], place, row_out.at[step], row_in.at[me], to, line, core
+            row_send.at[to, core], place, row_out.at[step], row_in.at[me], to, line, core
         ).start()
     pair_copy = remote(
-        weight_ref, pairs, pair_out.at[0], pair_in.at[0], me, line, 1 - core
+        weight, pairs, pair_out.at[0], pair_in.at[0], me, line, 1 - core
     )
     pair_copy.start()
 
@@ -229,41 +251,53 @@
     power[...] = jnp.zeros_like(power)
     cross[...] = jnp.zeros_like(cross)
 
-    for step in range(tile):
-        to = lax.rem(me + step, tile)
-        arrived(cols.at[:, pl.ds(pl.multiple_of(to * rows, rows), rows)], row_in.at[to])
-    mixed = jnp.dot(cols[...], wave[...], preferred_element_type=jnp.float32)
-    spec[0] = mixed[:freqs, :count] + mixed[freqs:, count:]
-    spec[1] = mixed[freqs:, :count] - mixed[:freqs, count:]
+    order = (
+        plane,
+        plane + 1 - 2 * lax.rem(plane, 2),
+        lax.rem(plane + planes // 2, planes),
+        planes - 1 - plane,
+    )
+    nearest = [at * width + shift for at in order for shift in range(width)]
+    for origin in nearest:
+        arrived(column_of(origin, core), row_in.at[origin])
+        shared(origin).start()
+    for origin in nearest:
+        arrived(column_of(origin, 1 - core), share_in.at[origin])
+    mixed = jnp.dot(
+        cols[...].reshape(2 * freqs, pixels), wave[...], preferred_element_type=jnp.float32
+    )
+    for other in range(cond):
+        re = mixed[2 * other * part : (2 * other + 1) * part]
+        im = mixed[(2 * other + 1) * part : (2 * other + 2) * part]
+        spec[0, other * part : (other + 1) * part] = re[:, :count] + im[:, count:]
+        spec[1, other * part : (other + 1) * part] = im[:, :count] - re[:, count:]
     kern_load.wait()
 
-    def targets():
-        for layer in range(conds):
-            for shift in range(width):
-                for other in range(cond):
-                    index = (layer * width + shift) * cond + other
-                    to = (core * conds + layer) * width + shift
-                    yield index, layer, shift, other, to, jnp.logical_and(to == me, other == core)
-
-    def filter_item(item):
-        for layer in range(conds):
-            for shift in range(width):
-                slot = shift * items + item
-                for at in range(0, freqs, pack):
-                    near = pl.ds(at, pack)
-                    kern_re = held[0, layer, slot, near, :].astype(jnp.float32)
-                    kern_im = held[1, layer, slot, near, :].astype(jnp.float32)
-                    spec_re = spec[0, near, :]
-                    spec_im = spec[1, near, :]
-                    filt[layer, slot, near, :count] = (
-                        spec_re * kern_re - spec_im * kern_im
-                    ).astype(jnp.bfloat16)
-                    filt[layer, slot, near, count:] = (
-                        spec_re * kern_im + spec_im * kern_re
-                    ).astype(jnp.bfloat16)
-
-    def send_item(item):
-        for index, layer, shift, other, to, mine in targets():
+    blocks = [(layer, shift) for layer in range(conds) for shift in range(width)]
+
+    def targets(layer, shift):
+        to = (core * conds + layer) * width + shift
+        for other in range(cond):
+            index = (layer * width + shift) * cond + other
+            yield index, other, to, jnp.logical_and(to == me, other == core)
+
+    def filter_block(item, layer, shift):
+        slot = shift * items + item
+        for at in range(0, freqs, pack):
+            near = pl.ds(at, pack)
+            kern_re = held[0, layer, slot, near, :].astype(jnp.float32)
+            kern_im = held[1, layer, slot, near, :].astype(jnp.float32)
+            spec_re = spec[0, near, :]
+            spec_im = spec[1, near, :]
+            filt[layer, slot, near, :count] = (spec_re * kern_re - spec_im * kern_im).astype(
+                jnp.bfloat16
+            )
+            filt[layer, slot, near, count:] = (spec_re * kern_im + spec_im * kern_re).astype(
+                jnp.bfloat16
+            )
+
+    def send_block(item, layer, shift):
+        for index, other, to, mine in targets(layer, shift):
             src = filt.at[layer, shift * items + item, pl.ds(other * part, part)]
             dst = recv.at[item, me, pl.ds(other * part, part)]
 
@@ -277,18 +311,24 @@
                     src, dst, send_out.at[item, index], send_in.at[item, me], to, line, other
                 ).start()
 
-    filter_item(0)
-
     def source_step(item, carry):
-        filter_item(item)
-        send_item(item - 1)
+        for index, block in enumerate(blocks):
+            filter_block(item, *block)
+            if index:
+                send_block(item, *blocks[index - 1])
+            else:
+
+                @pl.when(item > 0)
+                def _():
+                    send_block(item - 1, *blocks[-1])
+
         return carry
 
-    lax.fori_loop(1, items, source_step, 0)
-    send_item(items - 1)
+    lax.fori_loop(0, items, source_step, 0)
+    send_block(items - 1, *blocks[-1])
 
     pair_copy.wait()
-    weights = jnp.where(source == core, weight_ref[...], pairs[...])
+    weights = jnp.where(source == core, weight[...], pairs[...])
     lane = lax.broadcasted_iota(jnp.int32, weights.shape, 1)
     level = lax.broadcasted_iota(jnp.int32, weights.shape, 0)
     weights = jnp.where(level == lax.rem(plane, conds), weights, 0.0)
@@ -337,7 +377,7 @@
         half[...] = jnp.dot(
             recv[item].reshape(count, 2 * count), turn[...], preferred_element_type=jnp.float32
         ).astype(jnp.bfloat16)
-        weight = jnp.sum(jnp.where(lane == column * items + item, weights, 0.0))
+        scale = jnp.sum(jnp.where(lane == column * items + item, weights, 0.0))
 
         def pixel_step(step, carry):
             grid[...] = jnp.dot(back[step], half[...], preferred_element_type=jnp.float32)
@@ -350,10 +390,10 @@
                 b_re = grid[far, :lanes]
                 b_im = grid[far, lanes:]
                 into = pl.ds(pl.multiple_of(step * wide + at * pack, pack), pack)
-                power[into, :] += weight * (
+                power[into, :] += scale * (
                     (a_re * a_re + a_im * a_im) + (b_re * b_re + b_im * b_im)
                 )
-                cross[into, :] += weight * (a_im * b_re - a_re * b_im)
+                cross[into, :] += scale * (a_im * b_re - a_re * b_im)
                 return carry
 
             lax.fori_loop(0, wide // pack, group, 0)
@@ -368,9 +408,9 @@
                 a = a_re * a_re + a_im * a_im
                 b = b_re * b_re + b_im * b_im
                 only = lax.broadcasted_iota(jnp.int32, (top, lanes), 0) == 0
-                power[:top, :] -= jnp.where(only, (0.5 * weight) * (a + b), 0.0)
+                power[:top, :] -= jnp.where(only, (0.5 * scale) * (a + b), 0.0)
                 cross[:top, :] += jnp.where(
-                    only, weight * (0.25 * (a - b) - (a_im * b_re - a_re * b_im)), 0.0
+                    only, scale * (0.25 * (a - b) - (a_im * b_re - a_re * b_im)), 0.0
                 )
 
             @pl.when(item == items - 1)
@@ -461,21 +501,24 @@
                 for layer in range(planes)
             ]
             into = pl.ds(pl.multiple_of((core * subs + sub) * chunk + at, pack), pack)
-            final[0, into, :] = functools.reduce(jnp.minimum, values)
-            final[1, into, :] = functools.reduce(jnp.maximum, values)
+            final[0, into, :] = functools.reduce(jnp.minimum, values).astype(jnp.bfloat16)
+            final[1, into, :] = functools.reduce(jnp.maximum, values).astype(jnp.bfloat16)
         swap(sub).start()
 
     for step in range(1, tile):
         to = lax.rem(me + step, tile)
-        pltpu.make_async_copy(row_send.at[to], row_send.at[to], row_out.at[step]).wait()
+        arrived(row_send.at[to, core], row_out.at[step])
+    for origin in range(tile):
+        shared(origin).wait_send()
 
     def drain(item, carry):
-        for index, layer, shift, other, to, mine in targets():
-            src = filt.at[layer, shift * items + item, pl.ds(other * part, part)]
-
-            @pl.when(jnp.logical_not(mine))
-            def _():
-                arrived(src, send_out.at[item, index])
+        for layer, shift in blocks:
+            for index, other, to, mine in targets(layer, shift):
+                src = filt.at[layer, shift * items + item, pl.ds(other * part, part)]
+
+                @pl.when(jnp.logical_not(mine))
+                def _():
+                    arrived(src, send_out.at[item, index])
 
         for origin in range(tile):
             arrived(recv.at[item, origin, mine_half], pass_out.at[item, origin])
@@ -514,7 +557,7 @@
     dma = pltpu.SemaphoreType.DMA
     return pl.pallas_call(
         functools.partial(fused_kernel, sizes),
-        out_shape=jax.ShapeDtypeStruct((2, lanes, rows), jnp.float32),
+        out_shape=jax.ShapeDtypeStruct((2, lanes, rows), jnp.bfloat16),
         in_specs=[
             pl.BlockSpec(memory_space=pltpu.VMEM),
             pl.BlockSpec(memory_space=pltpu.VMEM),
@@ -525,8 +568,8 @@
         scratch_shapes=[
             pltpu.VMEM((pixels, 2 * count), jnp.bfloat16),
             pltpu.VMEM(kernels.shape, jnp.bfloat16),
-            pltpu.VMEM((tile, 2 * freqs, rows), jnp.bfloat16),
-            pltpu.VMEM((2 * freqs, pixels), jnp.bfloat16),
+            pltpu.VMEM((tile, cond, 2 * freqs // cond, rows), jnp.bfloat16),
+            pltpu.VMEM((cond, 2 * freqs // cond, pixels), jnp.bfloat16),
             pltpu.VMEM((2, freqs, count), jnp.float32),
             pltpu.VMEM((conds, kerns, freqs, 2 * count), jnp.bfloat16),
             pltpu.VMEM((items, tile, freqs, 2 * count), jnp.bfloat16),
@@ -536,12 +579,12 @@
             pltpu.VMEM((2 * wide, pixels), jnp.float32),
             pltpu.VMEM((lanes, lanes), jnp.float32),
             pltpu.VMEM((lanes, lanes), jnp.float32),
-            pltpu.VMEM(weights.shape, jnp.float32),
+            pltpu.VMEM((8, 128), jnp.float32),
             pltpu.VMEM((kern, width, lanes, lanes // width), jnp.bfloat16),
             pltpu.VMEM((peers, lanes, lanes // width), jnp.bfloat16),
             pltpu.VMEM((planes // cond, lanes, rows), jnp.bfloat16),
             pltpu.VMEM((planes, pieces // cond, chunk, rows), jnp.bfloat16),
-            pltpu.VMEM((2, lanes, rows), jnp.float32),
+            pltpu.VMEM((2, lanes, rows), jnp.bfloat16),
             dma((2,)),
             dma((tile,)),
             dma((tile,)),
@@ -557,6 +600,9 @@
             dma((planes, pieces // cond)),
             dma((pieces // cond,)),
             dma((pieces // cond,)),
+            dma((tile,)),
+            dma((tile,)),
+            pltpu.VMEM((8, 128), jnp.float32),
         ],
         compiler_params=pltpu.CompilerParams(
             collective_id=0, has_side_effects=True, vmem_limit_bytes=60 * 1024 * 1024
@@ -570,14 +616,13 @@
     slot = lax.broadcasted_iota(jnp.int32, (size, size), 0)
     pixel = lax.broadcasted_iota(jnp.int32, (size, size), 1)
     wanted = jnp.where(line == 0, pixel, jnp.where(pixel == 0, 0, size - pixel))
-    order = (slot == wanted).astype(jnp.float32)
+    order = (slot == wanted).astype(jnp.bfloat16)
     for ref, index in ((low_ref, 0), (high_ref, 1)):
         ref[0] = lax.dot_general(
             final_ref[index],
             order,
             (((0,), (0,)), ((), ())),
             preferred_element_type=jnp.float32,
-            precision=lax.Precision.HIGHEST,
         )
 
 
@@ -587,8 +632,7 @@
     conds, kerns = kernel_weights.shape
     cos, sin = host_tables(pixels, count)
     wave = jnp.asarray(np.concatenate([cos, sin], axis=1), jnp.bfloat16)
-    weights = jnp.pad(kernel_weights, ((0, 8 - conds), (0, 128 - kerns)))
-    final = fused(sizes, mask[0], kernels, weights, wave)
+    final = fused(sizes, mask[0], kernels, kernel_weights, wave)
     shape = jax.ShapeDtypeStruct((1, rows, pixels // 2), jnp.float32)
     return pl.pallas_call(place_kernel, out_shape=(shape, shape))(final)
 

time: 115 us -> 112 us (0.974)
  Pallas kernels: 113 us -> 111 us
  local copies, waits for them, and re-layouts: 1.28 us -> 0 us
    pad x1 -> x0, local copies, waits for them, and re-layouts: 1.28 us -> none  [planes_of(): weights = jnp.pad(kernel_weights, ((0, 8 - conds), (0, 128 - kerns)))]
where the time goes in v2:
time: 112 us
  Pallas kernels  111 us (99%)
    pallas_call x1, Pallas kernels, fused(): pl.pallas_call(functools.partial(fused_kernel, sizes), out_shape=jax.Shap...  109 us

profile of v2, /device:TPU:0, one launch (start us, length us, event | category | flops | bytes accessed | tf_op | source)
XLA Modules:
  0.0 112.1 jit_solution(149893782356809991)
XLA Ops:
  0.6 109.4 %shard_map.59.final_ref = bf16[2,512,128]{2,1,0:T(8,128)(2,1)} custom-call(bf16[128,1024]{1,0:T(8,128)(2,1)} %bitcast.1, f32[2,12]{1,0:T(2,128)} %weight_ref.1, bf16[1024,1024]{1,0:T(8,128)(2,1)} %constant.2.clone.wave_hbm, bf16[2,2,12,64,512]{4,3,2,1,0:T(8,128)(2,1)} %kern_hbm.1), custom_call_target="tpu_custom_call" | custom-call | tf_op jit(solution)/shard_map/pallas_call | solution.py:558
  110.1 2.0 %shard_map.60 = (f32[1,128,512]{2,1,0:T(8,128)}, f32[1,128,512]{2,1,0:T(8,128)}) custom-call(bf16[2,512,128]{2,1,0:T(8,128)(2,1)} %shard_map.59.final_ref), custom_call_target="tpu_custom_call" | custom-call | tf_op jit(solution)/shard_map/pallas_call | solution.py:637

commit v3 on v2

--- a/solution.py
+++ b/solution.py
@@ -114,16 +114,15 @@
 MESH = pl.DeviceIdType.MESH
 
 
-def fused_kernel(sizes, mask_ref, weight_ref, wave_hbm, kern_hbm, out_ref, *scratch):
+def fused_kernel(sizes, mask_hbm, weight_hbm, wave_hbm, kern_hbm, out_ref, *scratch):
     tile, kern, cond = sizes
     (wave, held, row_send, cols, spec, filt, recv, turn, back, half, grid, power, cross, pairs) = scratch[:14]
-    (quarter_send, quarter_recv, plane_send, plane_recv, final) = scratch[14:19]
-    weight = scratch[-1]
-    (load_sem, row_out, row_in, pair_out, pair_in, send_out, send_in, pass_out, pass_in) = scratch[19:28]
-    (quarter_out, quarter_in, plane_out, plane_in, final_out, final_in, share_out, share_in) = (
-        scratch[28:-1]
-    )
-    rows, pixels = mask_ref.shape
+    (quarter_send, quarter_recv, plane_send, plane_recv) = scratch[14:18]
+    weight, weight_ref, mask_ref = scratch[-3:]
+    (load_sem, row_out, row_in, share_out, share_in, pair_out, pair_in) = scratch[18:25]
+    (send_out, send_in, pass_out, pass_in) = scratch[25:29]
+    (quarter_out, quarter_in, plane_out, plane_in) = scratch[29:33]
+    rows, pixels = mask_hbm.shape
     _, conds, kerns, freqs, count = kern_hbm.shape
     planes = conds * cond
     width = tile // planes
@@ -134,7 +133,7 @@
     side = lanes // width
     steps = back.shape[0]
     chunk = plane_recv.shape[2]
-    subs = plane_recv.shape[1]
+    pieces = plane_recv.shape[1]
     me = lax.axis_index("tile")
     line = lax.axis_index("kern")
     core = lax.axis_index("cond")
@@ -154,11 +153,6 @@
 
     def arrived(ref, sem):
         pltpu.make_async_copy(ref, ref, sem).wait()
-
-    wave_load = pltpu.make_async_copy(wave_hbm, wave, load_sem.at[0])
-    kern_load = pltpu.make_async_copy(kern_hbm, held, load_sem.at[1])
-    wave_load.start()
-    kern_load.start()
 
     barrier = pltpu.get_barrier_semaphore()
     for step in range(tile - 1, 0, -1):
@@ -189,14 +183,25 @@
         )
     greeted = (tile - 1) * cond + 1 + width
 
-    weight[...] = jnp.zeros_like(weight)
-    weight[:conds, :kerns] = weight_ref[...]
+    wave_load = pltpu.make_async_copy(wave_hbm, wave, load_sem.at[0])
+    kern_load = pltpu.make_async_copy(kern_hbm, held, load_sem.at[1])
+    mask_load = pltpu.make_async_copy(mask_hbm, mask_ref, load_sem.at[2])
+    weight_load = pltpu.make_async_copy(weight_hbm, weight_ref, load_sem.at[3])
+    mask_load.start()
+    wave_load.start()
+    weight_load.start()
+    kern_load.start()
+
+    mask_load.wait()
     wave_load.wait()
     row = jnp.dot(mask_ref[...], wave[...], preferred_element_type=jnp.float32).T
     row_re = row[:count].reshape(tile, cond, part, rows).astype(jnp.bfloat16)
     row_im = (-row[count:]).reshape(tile, cond, part, rows).astype(jnp.bfloat16)
     row_send[:, :, :part, :] = row_re
     row_send[:, :, part:, :] = row_im
+    weight[...] = jnp.zeros_like(weight)
+    weight_load.wait()
+    weight[:conds, :kerns] = weight_ref[...]
 
     pl.semaphore_wait(barrier, greeted)
 
@@ -347,11 +352,7 @@
             1 - core,
         )
 
-    peers = []
-    for turn_x in range(width):
-        for turn_y in range(kern):
-            if turn_x or turn_y:
-                peers.append((turn_x, turn_y))
+    peers = [(1, 1), (1, 0), (0, 1)]
 
     def quarter(index, piece):
         turn_x, turn_y = peers[index]
@@ -369,14 +370,25 @@
         )
 
     def item_step(item, carry):
-        for origin in range(tile):
-            arrived(recv.at[item, origin, mine_half], send_in.at[item, origin])
-            passed(item, origin).start()
-        for origin in range(tile):
-            arrived(recv.at[item, origin, their_half], pass_in.at[item, origin])
-        half[...] = jnp.dot(
-            recv[item].reshape(count, 2 * count), turn[...], preferred_element_type=jnp.float32
-        ).astype(jnp.bfloat16)
+        def ready(index):
+            for shift in range(width):
+                origin = nearest[index * width + shift]
+                arrived(recv.at[item, origin, their_half], pass_in.at[item, origin])
+            first = order[index] * width
+            block = recv[item, pl.ds(first, width)].reshape(width * freqs, 2 * count)
+            into = pl.ds(pl.multiple_of(first * freqs, width * freqs), width * freqs)
+            half[into, :] = jnp.dot(
+                block, turn[...], preferred_element_type=jnp.float32
+            ).astype(jnp.bfloat16)
+
+        for index in range(planes):
+            for shift in range(width):
+                origin = nearest[index * width + shift]
+                arrived(recv.at[item, origin, mine_half], send_in.at[item, origin])
+                passed(item, origin).start()
+            if index:
+                ready(index - 1)
+        ready(planes - 1)
         scale = jnp.sum(jnp.where(lane == column * items + item, weights, 0.0))
 
         def pixel_step(step, carry):
@@ -444,24 +456,20 @@
 
     lax.fori_loop(0, items, item_step, 0)
 
-    def to_plane(layer, piece):
-        other = piece // subs
-        return (
+    def to_plane(layer, piece, other):
+        return remote(
             plane_send.at[layer, pl.ds(piece * chunk, chunk)],
-            plane_recv.at[plane, piece % subs],
-            plane_out.at[layer, piece],
-            plane_in.at[plane, piece % subs],
+            plane_recv.at[plane, piece],
+            plane_out.at[layer, piece, other],
+            plane_in.at[plane, piece],
             (core * (planes // cond) + layer) * width + column,
             line,
             other,
         )
 
-    def own_plane(layer, piece):
-        return jnp.logical_and(
-            core * (planes // cond) + layer == plane, piece // subs == core
-        )
-
-    pieces = subs * cond
+    def own_plane(layer, other):
+        return jnp.logical_and(core * (planes // cond) + layer == plane, other == core)
+
     own_side = pl.ds(pl.multiple_of(column * side, side), side)
     for piece in range(pieces):
         for index in range(len(peers)):
@@ -476,34 +484,19 @@
                     jnp.bfloat16
                 )
         for layer in range(planes // cond):
-            src, dst, out_sem, in_sem, to, to_line, other = to_plane(layer, piece)
-
-            @pl.when(own_plane(layer, piece))
-            def _():
-                pltpu.make_async_copy(src, dst, in_sem).start()
-
-            @pl.when(jnp.logical_not(own_plane(layer, piece)))
-            def _():
-                remote(src, dst, out_sem, in_sem, to, to_line, other).start()
-
-    def swap(sub):
-        span = pl.ds(pl.multiple_of((core * subs + sub) * chunk, chunk), chunk)
-        return remote(
-            final.at[:, span], final.at[:, span], final_out.at[sub], final_in.at[sub], me, line, 1 - core
-        )
-
-    for sub in range(subs):
-        for layer in range(planes):
-            arrived(plane_recv.at[layer, sub], plane_in.at[layer, sub])
-        for at in range(0, chunk, pack):
-            values = [
-                plane_recv[layer, sub, at : at + pack, :].astype(jnp.float32)
-                for layer in range(planes)
-            ]
-            into = pl.ds(pl.multiple_of((core * subs + sub) * chunk + at, pack), pack)
-            final[0, into, :] = functools.reduce(jnp.minimum, values).astype(jnp.bfloat16)
-            final[1, into, :] = functools.reduce(jnp.maximum, values).astype(jnp.bfloat16)
-        swap(sub).start()
+            for other in range(cond):
+
+                @pl.when(own_plane(layer, other))
+                def _():
+                    pltpu.make_async_copy(
+                        plane_send.at[layer, pl.ds(piece * chunk, chunk)],
+                        plane_recv.at[plane, piece],
+                        plane_in.at[plane, piece],
+                    ).start()
+
+                @pl.when(jnp.logical_not(own_plane(layer, other)))
+                def _():
+                    to_plane(layer, piece, other).start()
 
     for step in range(1, tile):
         to = lax.rem(me + step, tile)
@@ -529,16 +522,23 @@
         for index in range(len(peers)):
             quarter(index, piece).wait_send()
         for layer in range(planes // cond):
-
-            @pl.when(jnp.logical_not(own_plane(layer, piece)))
-            def _():
-                arrived(plane_send.at[layer, pl.ds(piece * chunk, chunk)], plane_out.at[layer, piece])
-
-    for sub in range(subs):
-        their = pl.ds(pl.multiple_of(((1 - core) * subs + sub) * chunk, chunk), chunk)
-        arrived(final.at[:, their], final_in.at[sub])
-        swap(sub).wait_send()
-    out_ref[...] = final[...]
+            for other in range(cond):
+
+                @pl.when(jnp.logical_not(own_plane(layer, other)))
+                def _():
+                    to_plane(layer, piece, other).wait_send()
+
+    for piece in range(pieces):
+        for layer in range(planes):
+            arrived(plane_recv.at[layer, piece], plane_in.at[layer, piece])
+        for at in range(0, chunk, pack):
+            values = [
+                plane_recv[layer, piece, at : at + pack, :].astype(jnp.float32)
+                for layer in range(planes)
+            ]
+            into = pl.ds(piece * chunk + at, pack)
+            out_ref[0, into, :] = functools.reduce(jnp.minimum, values).astype(jnp.bfloat16)
+            out_ref[1, into, :] = functools.reduce(jnp.maximum, values).astype(jnp.bfloat16)
 
 
 def fused(sizes, mask, kernels, weights, wave):
@@ -559,10 +559,10 @@
         functools.partial(fused_kernel, sizes),
         out_shape=jax.ShapeDtypeStruct((2, lanes, rows), jnp.bfloat16),
         in_specs=[
-            pl.BlockSpec(memory_space=pltpu.VMEM),
-            pl.BlockSpec(memory_space=pltpu.VMEM),
-            pl.BlockSpec(memory_space=pl.ANY),
-            pl.BlockSpec(memory_space=pl.ANY),
+            pl.BlockSpec(memory_space=pltpu.HBM),
+            pl.BlockSpec(memory_space=pltpu.HBM),
+            pl.BlockSpec(memory_space=pltpu.HBM),
+            pl.BlockSpec(memory_space=pltpu.HBM),
         ],
         out_specs=pl.BlockSpec(memory_space=pltpu.VMEM),
         scratch_shapes=[
@@ -583,9 +583,10 @@
             pltpu.VMEM((kern, width, lanes, lanes // width), jnp.bfloat16),
             pltpu.VMEM((peers, lanes, lanes // width), jnp.bfloat16),
             pltpu.VMEM((planes // cond, lanes, rows), jnp.bfloat16),
-            pltpu.VMEM((planes, pieces // cond, chunk, rows), jnp.bfloat16),
-            pltpu.VMEM((2, lanes, rows), jnp.bfloat16),
-            dma((2,)),
+            pltpu.VMEM((planes, pieces, chunk, rows), jnp.bfloat16),
+            dma((4,)),
+            dma((tile,)),
+            dma((tile,)),
             dma((tile,)),
             dma((tile,)),
             dma((1,)),
@@ -596,34 +597,34 @@
             dma((items, tile)),
             dma((pieces, peers)),
             dma((pieces, peers)),
-            dma((planes // cond, pieces)),
-            dma((planes, pieces // cond)),
-            dma((pieces // cond,)),
-            dma((pieces // cond,)),
-            dma((tile,)),
-            dma((tile,)),
+            dma((planes // cond, pieces, cond)),
+            dma((planes, pieces)),
             pltpu.VMEM((8, 128), jnp.float32),
+            pltpu.VMEM(weights.shape, jnp.float32),
+            pltpu.VMEM(mask.shape, jnp.bfloat16),
         ],
         compiler_params=pltpu.CompilerParams(
-            collective_id=0, has_side_effects=True, vmem_limit_bytes=60 * 1024 * 1024
+            collective_id=0, has_side_effects=True, vmem_limit_bytes=48 * 1024 * 1024
         ),
     )(mask, weights, wave, kernels)
 
 
-def place_kernel(final_ref, low_ref, high_ref):
+def place_kernel(final, low_hbm, high_hbm, placed, store_sem):
     line = lax.axis_index("kern")
-    size = final_ref.shape[1]
+    size = final.shape[1]
     slot = lax.broadcasted_iota(jnp.int32, (size, size), 0)
     pixel = lax.broadcasted_iota(jnp.int32, (size, size), 1)
     wanted = jnp.where(line == 0, pixel, jnp.where(pixel == 0, 0, size - pixel))
     order = (slot == wanted).astype(jnp.bfloat16)
-    for ref, index in ((low_ref, 0), (high_ref, 1)):
-        ref[0] = lax.dot_general(
-            final_ref[index],
-            order,
-            (((0,), (0,)), ((), ())),
-            preferred_element_type=jnp.float32,
+    stores = []
+    for index, target in enumerate((low_hbm, high_hbm)):
+        placed[index] = lax.dot_general(
+            final[index], order, (((0,), (0,)), ((), ())), preferred_element_type=jnp.float32
         )
+        stores.append(pltpu.make_async_copy(placed.at[index], target.at[0], store_sem.at[index]))
+        stores[-1].start()
+    for store in stores:
+        store.wait()
 
 
 def planes_of(sizes, mask, kernels, kernel_weights):
@@ -632,9 +633,26 @@
     conds, kerns = kernel_weights.shape
     cos, sin = host_tables(pixels, count)
     wave = jnp.asarray(np.concatenate([cos, sin], axis=1), jnp.bfloat16)
-    final = fused(sizes, mask[0], kernels, kernel_weights, wave)
+    final = fused(
+        sizes,
+        *(
+            pltpu.with_memory_space_constraint(value, pltpu.HBM)
+            for value in (mask[0], kernels, kernel_weights, wave)
+        ),
+    )
     shape = jax.ShapeDtypeStruct((1, rows, pixels // 2), jnp.float32)
-    return pl.pallas_call(place_kernel, out_shape=(shape, shape))(final)
+    anywhere = pl.BlockSpec(memory_space=pltpu.HBM)
+    return pl.pallas_call(
+        place_kernel,
+        out_shape=(shape, shape),
+        in_specs=[pl.BlockSpec(memory_space=pltpu.VMEM)],
+        out_specs=(anywhere, anywhere),
+        scratch_shapes=[
+            pltpu.VMEM((2, rows, pixels // 2), jnp.float32),
+            pltpu.SemaphoreType.DMA((2,)),
+        ],
+        compiler_params=pltpu.CompilerParams(vmem_limit_bytes=8 * 1024 * 1024),
+    )(final)
 
 
 def plan(mesh):

time: 112 us -> 108 us (0.964)
  Pallas kernels: 111 us -> 107 us
    pallas_call x1, Pallas kernels: 109 us -> 106 us  [fused(): pl.pallas_call(functools.partial(fused_kernel, sizes), out_shape=jax.Shap...]
where the time goes in v3:
time: 108 us
  Pallas kernels  107 us (99%)
    pallas_call x1, Pallas kernels, fused(): pl.pallas_call(functools.partial(fused_kernel, sizes), out_shape=jax.Shap...  106 us

profile of v3, /device:TPU:0, one launch (start us, length us, event | category | flops | bytes accessed | tf_op | source)
XLA Modules:
  0.0 108.1 jit_solution(6883920479213124759)
XLA Ops:
  0.6 106.4 %shard_map.59.final = bf16[2,512,128]{2,1,0:T(8,128)(2,1)S(1)} custom-call(bf16[128,1024]{1,0:T(8,128)(2,1)} %bitcast.1, f32[2,12]{1,0:T(2,128)} %weight_hbm.1, bf16[1024,1024]{1,0:T(8,128)(2,1)} %constant.2.clone.wave_hbm, bf16[2,2,12,64,512]{4,3,2,1,0:T(8,128)(2,1)} %kern_hbm.1), custom_call_target="tpu_custom_call" | custom-call | tf_op jit(solution)/shard_map/pallas_call | solution.py:558
  107.0 1.1 %shard_map.60 = (f32[1,128,512]{2,1,0:T(8,128)}, f32[1,128,512]{2,1,0:T(8,128)}) custom-call(bf16[2,512,128]{2,1,0:T(8,128)(2,1)S(1)} %shard_map.59.final), custom_call_target="tpu_custom_call" | custom-call | tf_op jit(solution)/shard_map/pallas_call | solution.py:645

commit v4 on v3

--- a/solution.py
+++ b/solution.py
@@ -117,11 +117,13 @@
 def fused_kernel(sizes, mask_hbm, weight_hbm, wave_hbm, kern_hbm, out_ref, *scratch):
     tile, kern, cond = sizes
     (wave, held, row_send, cols, spec, filt, recv, turn, back, half, grid, power, cross, pairs) = scratch[:14]
-    (quarter_send, quarter_recv, plane_send, plane_recv) = scratch[14:18]
+    (quarter_send, first_recv, second_send, second_recv, keep) = scratch[14:19]
+    (plane_send, plane_recv, final) = scratch[19:22]
     weight, weight_ref, mask_ref = scratch[-3:]
-    (load_sem, row_out, row_in, share_out, share_in, pair_out, pair_in) = scratch[18:25]
-    (send_out, send_in, pass_out, pass_in) = scratch[25:29]
-    (quarter_out, quarter_in, plane_out, plane_in) = scratch[29:33]
+    (load_sem, row_out, row_in, share_out, share_in, pair_out, pair_in) = scratch[22:29]
+    (send_out, send_in, pass_out, pass_in) = scratch[29:33]
+    (first_out, first_in, second_out, second_in) = scratch[33:37]
+    (plane_out, plane_in, final_out, final_in) = scratch[37:41]
     rows, pixels = mask_hbm.shape
     _, conds, kerns, freqs, count = kern_hbm.shape
     planes = conds * cond
@@ -231,6 +233,84 @@
     )
     pair_copy.start()
 
+    pack = 16
+
+    order = (
+        plane,
+        plane + 1 - 2 * lax.rem(plane, 2),
+        lax.rem(plane + planes // 2, planes),
+        planes - 1 - plane,
+    )
+    nearest = [at * width + shift for at in order for shift in range(width)]
+    for origin in nearest:
+        arrived(column_of(origin, core), row_in.at[origin])
+        shared(origin).start()
+    for origin in nearest:
+        arrived(column_of(origin, 1 - core), share_in.at[origin])
+    mixed = jnp.dot(
+        cols[...].reshape(2 * freqs, pixels), wave[...], preferred_element_type=jnp.float32
+    )
+    for other in range(cond):
+        re = mixed[2 * other * part : (2 * other + 1) * part]
+        im = mixed[(2 * other + 1) * part : (2 * other + 2) * part]
+        spec[0, other * part : (other + 1) * part] = re[:, :count] + im[:, count:]
+        spec[1, other * part : (other + 1) * part] = im[:, :count] - re[:, count:]
+    kern_load.wait()
+
+    blocks = [(layer, shift) for layer in range(conds) for shift in range(width)]
+
+    def targets(layer, shift):
+        to = (core * conds + layer) * width + shift
+        for other in range(cond):
+            index = (layer * width + shift) * cond + other
+            yield index, other, to, jnp.logical_and(to == me, other == core)
+
+    def filter_block(item, layer, shift):
+        slot = shift * items + item
+        for at in range(0, freqs, pack):
+            near = pl.ds(at, pack)
+            kern_re = held[0, layer, slot, near, :].astype(jnp.float32)
+            kern_im = held[1, layer, slot, near, :].astype(jnp.float32)
+            spec_re = spec[0, near, :]
+            spec_im = spec[1, near, :]
+            filt[layer, slot, near, :count] = (spec_re * kern_re - spec_im * kern_im).astype(
+                jnp.bfloat16
+            )
+            filt[layer, slot, near, count:] = (spec_re * kern_im + spec_im * kern_re).astype(
+                jnp.bfloat16
+            )
+
+    def send_block(item, layer, shift):
+        for index, other, to, mine in targets(layer, shift):
+            src = filt.at[layer, shift * items + item, pl.ds(other * part, part)]
+            dst = recv.at[item, me, pl.ds(other * part, part)]
+
+            @pl.when(mine)
+            def _():
+                pltpu.make_async_copy(src, dst, send_in.at[item, me]).start()
+
+            @pl.when(jnp.logical_not(mine))
+            def _():
+                remote(
+                    src, dst, send_out.at[item, index], send_in.at[item, me], to, line, other
+                ).start()
+
+    def source_step(item, carry):
+        for index, block in enumerate(blocks):
+            filter_block(item, *block)
+            if index:
+                send_block(item, *blocks[index - 1])
+            else:
+
+                @pl.when(item > 0)
+                def _():
+                    send_block(item - 1, *blocks[-1])
+
+        return carry
+
+    lax.fori_loop(0, items, source_step, 0)
+    send_block(items - 1, *blocks[-1])
+
     for shift in range(width):
         for layer in range(planes // cond):
             at = pl.multiple_of(
@@ -245,7 +325,6 @@
     for step in range(steps):
         back[step, :wide, :] = wave[step * wide : (step + 1) * wide, :count]
         back[step, wide:, :] = wave[step * wide : (step + 1) * wide, count:]
-    pack = 16
     first = lax.broadcasted_iota(jnp.int32, (pack, count), 0) == 0
     middle = jnp.broadcast_to(
         wave[pixels // 2 : pixels // 2 + pack, :count].astype(jnp.float32)[:1], (pack, count)
@@ -255,82 +334,6 @@
     ).astype(jnp.bfloat16)
     power[...] = jnp.zeros_like(power)
     cross[...] = jnp.zeros_like(cross)
-
-    order = (
-        plane,
-        plane + 1 - 2 * lax.rem(plane, 2),
-        lax.rem(plane + planes // 2, planes),
-        planes - 1 - plane,
-    )
-    nearest = [at * width + shift for at in order for shift in range(width)]
-    for origin in nearest:
-        arrived(column_of(origin, core), row_in.at[origin])
-        shared(origin).start()
-    for origin in nearest:
-        arrived(column_of(origin, 1 - core), share_in.at[origin])
-    mixed = jnp.dot(
-        cols[...].reshape(2 * freqs, pixels), wave[...], preferred_element_type=jnp.float32
-    )
-    for other in range(cond):
-        re = mixed[2 * other * part : (2 * other + 1) * part]
-        im = mixed[(2 * other + 1) * part : (2 * other + 2) * part]
-        spec[0, other * part : (other + 1) * part] = re[:, :count] + im[:, count:]
-        spec[1, other * part : (other + 1) * part] = im[:, :count] - re[:, count:]
-    kern_load.wait()
-
-    blocks = [(layer, shift) for layer in range(conds) for shift in range(width)]
-
-    def targets(layer, shift):
-        to = (core * conds + layer) * width + shift
-        for other in range(cond):
-            index = (layer * width + shift) * cond + other
-            yield index, other, to, jnp.logical_and(to == me, other == core)
-
-    def filter_block(item, layer, shift):
-        slot = shift * items + item
-        for at in range(0, freqs, pack):
-            near = pl.ds(at, pack)
-            kern_re = held[0, layer, slot, near, :].astype(jnp.float32)
-            kern_im = held[1, layer, slot, near, :].astype(jnp.float32)
-            spec_re = spec[0, near, :]
-            spec_im = spec[1, near, :]
-            filt[layer, slot, near, :count] = (spec_re * kern_re - spec_im * kern_im).astype(
-                jnp.bfloat16
-            )
-            filt[layer, slot, near, count:] = (spec_re * kern_im + spec_im * kern_re).astype(
-                jnp.bfloat16
-            )
-
-    def send_block(item, layer, shift):
-        for index, other, to, mine in targets(layer, shift):
-            src = filt.at[layer, shift * items + item, pl.ds(other * part, part)]
-            dst = recv.at[item, me, pl.ds(other * part, part)]
-
-            @pl.when(mine)
-            def _():
-                pltpu.make_async_copy(src, dst, send_in.at[item, me]).start()
-
-            @pl.when(jnp.logical_not(mine))
-            def _():
-                remote(
-                    src, dst, send_out.at[item, index], send_in.at[item, me], to, line, other
-                ).start()
-
-    def source_step(item, carry):
-        for index, block in enumerate(blocks):
-            filter_block(item, *block)
-            if index:
-                send_block(item, *blocks[index - 1])
-            else:
-
-                @pl.when(item > 0)
-                def _():
-                    send_block(item - 1, *blocks[-1])
-
-        return carry
-
-    lax.fori_loop(0, items, source_step, 0)
-    send_block(items - 1, *blocks[-1])
 
     pair_copy.wait()
     weights = jnp.where(source == core, weight[...], pairs[...])
@@ -352,22 +355,34 @@
             1 - core,
         )
 
-    peers = [(1, 1), (1, 0), (0, 1)]
-
-    def quarter(index, piece):
-        turn_x, turn_y = peers[index]
-        to_column = lax.rem(column + turn_x, width)
-        to_line = lax.rem(line + turn_y, kern)
+    def first(piece):
         span = pl.ds(piece * chunk, chunk)
+        along_x = piece % 2 == 0
         return remote(
-            quarter_send.at[to_line, to_column, span],
-            quarter_recv.at[index, span],
-            quarter_out.at[piece, index],
-            quarter_in.at[piece, index],
-            plane * width + to_column,
-            to_line,
+            quarter_send.at[:, 1 - column, span] if along_x else quarter_send.at[1 - line, :, span],
+            first_recv.at[:, span],
+            first_out.at[piece],
+            first_in.at[piece],
+            plane * width + (1 - column) if along_x else me,
+            line if along_x else 1 - line,
             core,
         )
+
+    def second(piece):
+        span = pl.ds(piece * chunk, chunk)
+        along_x = piece % 2 == 1
+        return remote(
+            second_send.at[span],
+            second_recv.at[span],
+            second_out.at[piece],
+            second_in.at[piece],
+            plane * width + (1 - column) if along_x else me,
+            line if along_x else 1 - line,
+            core,
+        )
+
+    ahead = 4
+    lag = 3
 
     def item_step(item, carry):
         def ready(index):
@@ -446,8 +461,13 @@
                         return carry
 
                     lax.fori_loop(0, chunk // pack, finish, 0)
-                    for index in range(len(peers)):
-                        quarter(index, step * (wide // chunk) + piece).start()
+
+                    for begun in range(steps):
+
+                        @pl.when(step == begun)
+                        def _():
+                            if begun * (wide // chunk) + piece < ahead:
+                                first(begun * (wide // chunk) + piece).start()
 
             return carry
 
@@ -455,6 +475,11 @@
         return carry
 
     lax.fori_loop(0, items, item_step, 0)
+
+    both = pieces - 0
+
+    def owners(piece):
+        return range(cond) if piece >= both else (piece % cond,)
 
     def to_plane(layer, piece, other):
         return remote(
@@ -471,20 +496,36 @@
         return jnp.logical_and(core * (planes // cond) + layer == plane, other == core)
 
     own_side = pl.ds(pl.multiple_of(column * side, side), side)
-    for piece in range(pieces):
-        for index in range(len(peers)):
-            arrived(quarter_recv.at[index, pl.ds(piece * chunk, chunk)], quarter_in.at[piece, index])
+    their_side = pl.ds(pl.multiple_of((1 - column) * side, side), side)
+
+    def combine(piece):
+        arrived(first_recv.at[:, pl.ds(piece * chunk, chunk)], first_in.at[piece])
         for at in range(piece * chunk, (piece + 1) * chunk, pack):
             span = pl.ds(at, pack)
-            total = power[span, own_side] + sign * cross[span, own_side]
-            for index in range(len(peers)):
-                total = total + quarter_recv[index, span, :].astype(jnp.float32)
+            kept = power[span, own_side] + sign * cross[span, own_side]
+            if piece % 2 == 0:
+                given = power[span, own_side] - sign * cross[span, own_side]
+                index = line
+            else:
+                given = power[span, their_side] + sign * cross[span, their_side]
+                index = column
+            keep[span, :] = kept + first_recv[index, span, :].astype(jnp.float32)
+            second_send[span, :] = (
+                given + first_recv[1 - index, span, :].astype(jnp.float32)
+            ).astype(jnp.bfloat16)
+        second(piece).start()
+
+    def complete(piece):
+        arrived(second_recv.at[pl.ds(piece * chunk, chunk)], second_in.at[piece])
+        for at in range(piece * chunk, (piece + 1) * chunk, pack):
+            span = pl.ds(at, pack)
+            total = keep[span, :] + second_recv[span, :].astype(jnp.float32)
             for layer in range(planes // cond):
                 plane_send[layer, span, :] = total[:, layer * rows : (layer + 1) * rows].astype(
                     jnp.bfloat16
                 )
         for layer in range(planes // cond):
-            for other in range(cond):
+            for other in owners(piece):
 
                 @pl.when(own_plane(layer, other))
                 def _():
@@ -498,37 +539,15 @@
                 def _():
                     to_plane(layer, piece, other).start()
 
-    for step in range(1, tile):
-        to = lax.rem(me + step, tile)
-        arrived(row_send.at[to, core], row_out.at[step])
-    for origin in range(tile):
-        shared(origin).wait_send()
-
-    def drain(item, carry):
-        for layer, shift in blocks:
-            for index, other, to, mine in targets(layer, shift):
-                src = filt.at[layer, shift * items + item, pl.ds(other * part, part)]
-
-                @pl.when(jnp.logical_not(mine))
-                def _():
-                    arrived(src, send_out.at[item, index])
-
-        for origin in range(tile):
-            arrived(recv.at[item, origin, mine_half], pass_out.at[item, origin])
-        return carry
-
-    lax.fori_loop(0, items, drain, 0)
-    for piece in range(pieces):
-        for index in range(len(peers)):
-            quarter(index, piece).wait_send()
-        for layer in range(planes // cond):
-            for other in range(cond):
-
-                @pl.when(jnp.logical_not(own_plane(layer, other)))
-                def _():
-                    to_plane(layer, piece, other).wait_send()
-
-    for piece in range(pieces):
+    for piece in range(pieces + lag):
+        if piece < pieces:
+            combine(piece)
+            if piece + ahead < pieces:
+                first(piece + ahead).start()
+        if piece >= lag:
+            complete(piece - lag)
+
+    def reduce(piece):
         for layer in range(planes):
             arrived(plane_recv.at[layer, piece], plane_in.at[layer, piece])
         for at in range(0, chunk, pack):
@@ -536,9 +555,63 @@
                 plane_recv[layer, piece, at : at + pack, :].astype(jnp.float32)
                 for layer in range(planes)
             ]
-            into = pl.ds(piece * chunk + at, pack)
-            out_ref[0, into, :] = functools.reduce(jnp.minimum, values).astype(jnp.bfloat16)
-            out_ref[1, into, :] = functools.reduce(jnp.maximum, values).astype(jnp.bfloat16)
+            into = pl.ds(pl.multiple_of(piece * chunk + at, pack), pack)
+            final[0, into, :] = functools.reduce(jnp.minimum, values).astype(jnp.bfloat16)
+            final[1, into, :] = functools.reduce(jnp.maximum, values).astype(jnp.bfloat16)
+
+    def swap(pair):
+        span = pl.ds(pl.multiple_of((pair * cond + core) * chunk, chunk), chunk)
+        return remote(
+            final.at[:, span],
+            final.at[:, span],
+            final_out.at[pair],
+            final_in.at[pair],
+            me,
+            line,
+            1 - core,
+        )
+
+    for pair in range(both // cond):
+        reduce(pair * cond + core)
+        swap(pair).start()
+    for piece in range(both, pieces):
+        reduce(piece)
+
+    for step in range(1, tile):
+        to = lax.rem(me + step, tile)
+        arrived(row_send.at[to, core], row_out.at[step])
+    for origin in range(tile):
+        shared(origin).wait_send()
+
+    def drain(item, carry):
+        for layer, shift in blocks:
+            for index, other, to, mine in targets(layer, shift):
+                src = filt.at[layer, shift * items + item, pl.ds(other * part, part)]
+
+                @pl.when(jnp.logical_not(mine))
+                def _():
+                    arrived(src, send_out.at[item, index])
+
+        for origin in range(tile):
+            arrived(recv.at[item, origin, mine_half], pass_out.at[item, origin])
+        return carry
+
+    lax.fori_loop(0, items, drain, 0)
+    for piece in range(pieces):
+        first(piece).wait_send()
+        second(piece).wait_send()
+        for layer in range(planes // cond):
+            for other in owners(piece):
+
+                @pl.when(jnp.logical_not(own_plane(layer, other)))
+                def _():
+                    to_plane(layer, piece, other).wait_send()
+
+    for pair in range(both // cond):
+        theirs = pl.ds(pl.multiple_of((pair * cond + 1 - core) * chunk, chunk), chunk)
+        arrived(final.at[:, theirs], final_in.at[pair])
+        swap(pair).wait_send()
+    out_ref[...] = final[...]
 
 
 def fused(sizes, mask, kernels, weights, wave):
@@ -553,7 +626,6 @@
     chunk = 128
     steps = lanes // wide
     pieces = lanes // chunk
-    peers = width * kern - 1
     dma = pltpu.SemaphoreType.DMA
     return pl.pallas_call(
         functools.partial(fused_kernel, sizes),
@@ -581,9 +653,13 @@
             pltpu.VMEM((lanes, lanes), jnp.float32),
             pltpu.VMEM((8, 128), jnp.float32),
             pltpu.VMEM((kern, width, lanes, lanes // width), jnp.bfloat16),
-            pltpu.VMEM((peers, lanes, lanes // width), jnp.bfloat16),
+            pltpu.VMEM((2, lanes, lanes // width), jnp.bfloat16),
+            pltpu.VMEM((lanes, lanes // width), jnp.bfloat16),
+            pltpu.VMEM((lanes, lanes // width), jnp.bfloat16),
+            pltpu.VMEM((lanes, lanes // width), jnp.float32),
             pltpu.VMEM((planes // cond, lanes, rows), jnp.bfloat16),
             pltpu.VMEM((planes, pieces, chunk, rows), jnp.bfloat16),
+            pltpu.VMEM((2, lanes, rows), jnp.bfloat16),
             dma((4,)),
             dma((tile,)),
             dma((tile,)),
@@ -595,10 +671,14 @@
             dma((items, tile)),
             dma((items, tile)),
             dma((items, tile)),
-            dma((pieces, peers)),
-            dma((pieces, peers)),
+            dma((pieces,)),
+            dma((pieces,)),
+            dma((pieces,)),
+            dma((pieces,)),
             dma((planes // cond, pieces, cond)),
             dma((planes, pieces)),
+            dma((pieces // cond,)),
+            dma((pieces // cond,)),
             pltpu.VMEM((8, 128), jnp.float32),
             pltpu.VMEM(weights.shape, jnp.float32),
             pltpu.VMEM(mask.shape, jnp.bfloat16),

time: 108 us -> 108 us (level)
  no operation moved by 1% of the time
where the time goes in v4:
time: 108 us
  Pallas kernels  107 us (99%)
    pallas_call x1, Pallas kernels, fused(): pl.pallas_call(functools.partial(fused_kernel, sizes), out_shape=jax.Shap...  106 us

profile of v4, /device:TPU:0, one launch (start us, length us, event | category | flops | bytes accessed | tf_op | source)
XLA Modules:
  0.0 108.0 jit_solution(9055768211672875617)
XLA Ops:
  0.6 106.2 %shard_map.59.final = bf16[2,512,128]{2,1,0:T(8,128)(2,1)S(1)} custom-call(bf16[128,1024]{1,0:T(8,128)(2,1)} %bitcast.1, f32[2,12]{1,0:T(2,128)} %weight_hbm.1, bf16[1024,1024]{1,0:T(8,128)(2,1)} %constant.2.clone.wave_hbm, bf16[2,2,12,64,512]{4,3,2,1,0:T(8,128)(2,1)} %kern_hbm.1), custom_call_target="tpu_custom_call" | custom-call | tf_op jit(solution)/shard_map/pallas_call | solution.py:630
  106.9 1.1 %shard_map.60 = (f32[1,128,512]{2,1,0:T(8,128)}, f32[1,128,512]{2,1,0:T(8,128)}) custom-call(bf16[2,512,128]{2,1,0:T(8,128)(2,1)S(1)} %shard_map.59.final), custom_call_target="tpu_custom_call" | custom-call | tf_op jit(solution)/shard_map/pallas_call | solution.py:725
